TPU v7x, 32 devices: a whole 2x2x4 slice. The times are simulated.
32 devices in a mesh: gx: 4 (over z), gy: 4 (over y, x), gz: 2 (over core).
Axes of the slice: x: 2, y: 2, z: 4, core: 2. Of those that a mesh axis runs over, the one named last changes fastest.
Arguments:
- patch_logits: bfloat16 [4, 4, 2, 24, 20736], P('gx', 'gy', 'gz'), may hold values from -12 to 312
- patch_start: int32 [4, 4, 2, 3], replicated, may hold values from 0 to 112, as said below
- patch_owner: int32 [4, 4, 2], replicated, may hold values from 0 to 15, as said below
Outputs:
- probs: float32 [32, 128, 3, 256], P('gx', 'gy', None, 'gz')
Inputs may be any that keep to these rules, and one draw needn't show every extreme that they name: `patch_start`: entry [i, j, k, d] is the first cell along dimension d of the patch at lattice position (i, j, k): i * 8 - 8 along x (32 and 128 in place of 8 along y and z), moved by at most 4 cells, then moved inward so that the patch lies inside the volume. `patch_owner`: for every k the entries [:, :, k] are the numbers 0 to 15, each once.
All inputs are finite; a program needn't handle non-finite values.
Results may differ from a plain program's by a relative error of at most 0.0003.
Values may be sent and summed in bfloat16 or wider, within the bound.
A program may use at most 128 MiB of HBM per device.

v0:
```python
import jax
import jax.numpy as jnp
from jax import lax
from jax.sharding import PartitionSpec as P

CLASSES = 3
BX = 8
BY = 32
BZ = 128
HALO = 8
PX = 24
PY = 48
PZ = 144


def extended(x, sides, width):
    for axis, dim in sides:
        size, length = (lax.axis_size(axis), x.shape[dim])
        up = [(i, (i + 1) % size) for i in range(size - 1)]
        down = [(j, i) for i, j in up]
        last = lax.slice_in_dim(x, length - width, length, axis=dim)
        first = lax.slice_in_dim(x, 0, width, axis=dim)
        before = lax.ppermute(last, axis, up)
        after = lax.ppermute(first, axis, down)
        x = jnp.concatenate([before, x, after], axis=dim)
    return x


def profile(offsets, length):
    inside = (offsets >= 0) & (offsets < length)
    centre = (length - 1) / 2.0
    spread = length / 4.0
    values = jnp.exp(-((offsets.astype(jnp.float32) - centre) ** 2) / (2.0 * spread * spread))
    return jnp.where(inside, values, 0.0)


def fold_rims(padded, block_len, margin):
    centre = padded[..., 2 * margin : 2 * margin + block_len]
    below_rim = padded[..., :margin]
    above_rim = padded[..., block_len + 3 * margin :]
    widths_low = [(0, 0)] * (padded.ndim - 1) + [(0, block_len - margin)]
    widths_high = [(0, 0)] * (padded.ndim - 1) + [(block_len - margin, 0)]
    return centre + jnp.pad(below_rim, widths_low) + jnp.pad(above_rim, widths_high)


def finish(canvas, classes):
    padded = extended(canvas, (("gz", 3),), 2 * HALO)
    summed = fold_rims(padded, BZ, 2 * HALO)
    scores = summed[:, :, :classes] / summed[:, :, classes:]
    return jax.nn.softmax(scores, axis=2)


def pad_patch(source, margin):
    return jnp.pad(source, ((BX, BX), (BY, BY), (0, 0), (margin, 2 * margin)))


def owner_block(padded, target, lanes_y, corner, shift_z, window):
    start_x = jnp.clip(target // lanes_y * BX - corner[0] + BX, 0, PX + BX)
    start_y = jnp.clip(target % lanes_y * BY - corner[1] + BY, 0, PY + BY)
    start_z = 2 * HALO - shift_z
    return lax.dynamic_slice(
        padded, (start_x, start_y, jnp.int32(0), start_z), (BX, BY, padded.shape[2], window)
    )


def per_device(patch_logits, patch_start, patch_owner):
    lanes_x = lax.axis_size("gx")
    lanes_y = lax.axis_size("gy")
    place_x = lax.axis_index("gx")
    place_y = lax.axis_index("gy")
    place_z = lax.axis_index("gz")
    classes = CLASSES
    logits = patch_logits[0, 0, 0].reshape(PX, PY, classes, PZ)
    margin = 2 * HALO
    window = BZ + 2 * margin
    anchor_x = place_x * BX
    anchor_y = place_y * BY
    anchor_z = place_z * BZ
    window_z = anchor_z - margin
    owners = lanes_x * lanes_y
    patch_code = patch_owner[place_x, place_y, place_z]
    corner = patch_start[patch_code // lanes_y, patch_code % lanes_y, place_z]
    shift_z = corner[2] - window_z
    padded = pad_patch(logits, margin)
    slot_ids = jnp.arange(owners)
    slot_data = jax.vmap(
        lambda target: owner_block(padded, target, lanes_y, corner, shift_z, window)
    )(slot_ids)
    arrived = lax.all_to_all(slot_data, ("gx", "gy"), split_axis=0, concat_axis=0, tiled=True)
    source_codes = patch_owner[:, :, place_z].reshape(owners)
    corners = patch_start[source_codes // lanes_y, source_codes % lanes_y, place_z]
    along_x = profile(anchor_x + jnp.arange(BX)[None, :] - corners[:, 0:1], PX)
    along_y = profile(anchor_y + jnp.arange(BY)[None, :] - corners[:, 1:2], PY)
    along_z = profile(window_z + jnp.arange(window)[None, :] - corners[:, 2:3], PZ)
    weight = along_x[:, :, None, None] * along_y[:, None, :, None]
    weight = weight * along_z[:, None, None, :]
    canvas = jnp.sum(arrived * weight[:, :, :, None, :], axis=0)
    canvas = jnp.concatenate([canvas, jnp.sum(weight, axis=0)[:, :, None, :]], axis=2)
    return finish(canvas, classes)


def solution(mesh):
    return jax.shard_map(
        per_device,
        mesh=mesh,
        in_specs=(P("gx", "gy", "gz", None, None), P(), P()),
        out_specs=P("gx", "gy", None, "gz"),
        check_vma=False,
    )
```

profile of v0, /device:TPU:12, one launch (start us, length us, event | category | flops | bytes accessed | tf_op | source)
XLA Modules:
  0.0 265.2 jit_solution(2288092240220715672)
XLA Ops:
  0.0 1.3 dynamic_slice.9
  3.9 1.4 fusion.44
  6.0 4.0 %reshape_squeeze.6 = bf16[24,48,3,144]{3,2,1,0:T(4,128)(2,1)S(1)} reshape(bf16[1,1,1,24,20736]{4,3,2,1,0:T(8,128)(2,1)} %param.3) | data formatting | bytes 1990656 | tf_op jit(solution)/shard_map/reshape;squeeze | solution.py:73
  10.0 1.2 compare_select_fusion.2
  11.2 13.3 %pad.12 = bf16[40,112,3,192]{3,2,1,0:T(4,128)(2,1)} pad(bf16[24,48,3,144]{3,2,1,0:T(4,128)(2,1)S(1)} %reshape_squeeze.6, bf16[]{:T(256)} %constant.106.clone.1), padding=8_8x32_32x0_0x16_32 | pad | bytes 6156290 | tf_op jit(solution)/shard_map/jit(_pad)/pad | solution.py:54
  24.6 76.8 %while.1 = (s32[]{:T(128)}, bf16[40,112,3,192]{3,2,1,0:T(4,128)(2,1)}, s32[16,4]{0,1:T(4,128)S(1)}, bf16[16,8,32,3,160]{4,2,3,1,0:T(8,128)(2,1)}, s32[]{:T(128)}) while((s32[]{:T(128)}, bf16[40,112,3,192]{3,2,1,0:T(4,128)(2,1)}, s32[16,4]{0,1:T(4,128)S(1)}, bf16[16,8,32,3,160]{4,2,3,1,0:T(8,128)(2,1)}, s32[]{:T(128)}) %tuple.28), condition=%wide.while_cond, body=%wide.while_body.sunk | while | flops 2 | bytes 1131141 | solution.py:61
  24.6 0.6 fusion.47
  25.2 3.3 %dynamic-slice_bitcast_fusion.2 = bf16[1,8,32,3,160]{4,3,2,1,0:T(4,128)(2,1)S(1)} fusion(bf16[40,112,3,192]{3,2,1,0:T(4,128)(2,1)} %get-tuple-element.80, s32[]{:T(128)} %bitcast.20, s32[]{:T(128)} %bitcast.21, s32[]{:T(128)} %bitcast.22), kind=kLoop, calls=%fused_computation.1.clone.1 | loop fusion | bytes 491532 | tf_op jit(solution)/shard_map/vmap()/gather
  28.5 0.8 copy_dynamic-update-slice_fusion.2
  29.4 0.6 fusion.47
  30.0 3.3 %dynamic-slice_bitcast_fusion.2 = bf16[1,8,32,3,160]{4,3,2,1,0:T(4,128)(2,1)S(1)} fusion(bf16[40,112,3,192]{3,2,1,0:T(4,128)(2,1)} %get-tuple-element.80, s32[]{:T(128)} %bitcast.20, s32[]{:T(128)} %bitcast.21, s32[]{:T(128)} %bitcast.22), kind=kLoop, calls=%fused_computation.1.clone.1 | loop fusion | bytes 491532 | tf_op jit(solution)/shard_map/vmap()/gather
  33.3 0.8 copy_dynamic-update-slice_fusion.2
  34.2 0.6 fusion.47
  34.8 3.3 %dynamic-slice_bitcast_fusion.2 = bf16[1,8,32,3,160]{4,3,2,1,0:T(4,128)(2,1)S(1)} fusion(bf16[40,112,3,192]{3,2,1,0:T(4,128)(2,1)} %get-tuple-element.80, s32[]{:T(128)} %bitcast.20, s32[]{:T(128)} %bitcast.21, s32[]{:T(128)} %bitcast.22), kind=kLoop, calls=%fused_computation.1.clone.1 | loop fusion | bytes 491532 | tf_op jit(solution)/shard_map/vmap()/gather
  38.1 0.8 copy_dynamic-update-slice_fusion.2
  39.0 0.6 fusion.47
  39.6 3.3 %dynamic-slice_bitcast_fusion.2 = bf16[1,8,32,3,160]{4,3,2,1,0:T(4,128)(2,1)S(1)} fusion(bf16[40,112,3,192]{3,2,1,0:T(4,128)(2,1)} %get-tuple-element.80, s32[]{:T(128)} %bitcast.20, s32[]{:T(128)} %bitcast.21, s32[]{:T(128)} %bitcast.22), kind=kLoop, calls=%fused_computation.1.clone.1 | loop fusion | bytes 491532 | tf_op jit(solution)/shard_map/vmap()/gather
  42.9 0.9 copy_dynamic-update-slice_fusion.2
  43.8 0.6 fusion.47
  44.4 3.3 %dynamic-slice_bitcast_fusion.2 = bf16[1,8,32,3,160]{4,3,2,1,0:T(4,128)(2,1)S(1)} fusion(bf16[40,112,3,192]{3,2,1,0:T(4,128)(2,1)} %get-tuple-element.80, s32[]{:T(128)} %bitcast.20, s32[]{:T(128)} %bitcast.21, s32[]{:T(128)} %bitcast.22), kind=kLoop, calls=%fused_computation.1.clone.1 | loop fusion | bytes 491532 | tf_op jit(solution)/shard_map/vmap()/gather
  47.7 0.8 copy_dynamic-update-slice_fusion.2
  48.6 0.6 fusion.47
  49.2 3.3 %dynamic-slice_bitcast_fusion.2 = bf16[1,8,32,3,160]{4,3,2,1,0:T(4,128)(2,1)S(1)} fusion(bf16[40,112,3,192]{3,2,1,0:T(4,128)(2,1)} %get-tuple-element.80, s32[]{:T(128)} %bitcast.20, s32[]{:T(128)} %bitcast.21, s32[]{:T(128)} %bitcast.22), kind=kLoop, calls=%fused_computation.1.clone.1 | loop fusion | bytes 491532 | tf_op jit(solution)/shard_map/vmap()/gather
  52.5 0.9 copy_dynamic-update-slice_fusion.2
  53.5 0.6 fusion.47
  54.0 3.3 %dynamic-slice_bitcast_fusion.2 = bf16[1,8,32,3,160]{4,3,2,1,0:T(4,128)(2,1)S(1)} fusion(bf16[40,112,3,192]{3,2,1,0:T(4,128)(2,1)} %get-tuple-element.80, s32[]{:T(128)} %bitcast.20, s32[]{:T(128)} %bitcast.21, s32[]{:T(128)} %bitcast.22), kind=kLoop, calls=%fused_computation.1.clone.1 | loop fusion | bytes 491532 | tf_op jit(solution)/shard_map/vmap()/gather
  57.4 0.8 copy_dynamic-update-slice_fusion.2
  58.2 0.6 fusion.47
  58.8 3.3 %dynamic-slice_bitcast_fusion.2 = bf16[1,8,32,3,160]{4,3,2,1,0:T(4,128)(2,1)S(1)} fusion(bf16[40,112,3,192]{3,2,1,0:T(4,128)(2,1)} %get-tuple-element.80, s32[]{:T(128)} %bitcast.20, s32[]{:T(128)} %bitcast.21, s32[]{:T(128)} %bitcast.22), kind=kLoop, calls=%fused_computation.1.clone.1 | loop fusion | bytes 491532 | tf_op jit(solution)/shard_map/vmap()/gather
  62.1 0.8 copy_dynamic-update-slice_fusion.2
  63.1 0.6 fusion.47
  63.6 3.3 %dynamic-slice_bitcast_fusion.2 = bf16[1,8,32,3,160]{4,3,2,1,0:T(4,128)(2,1)S(1)} fusion(bf16[40,112,3,192]{3,2,1,0:T(4,128)(2,1)} %get-tuple-element.80, s32[]{:T(128)} %bitcast.20, s32[]{:T(128)} %bitcast.21, s32[]{:T(128)} %bitcast.22), kind=kLoop, calls=%fused_computation.1.clone.1 | loop fusion | bytes 491532 | tf_op jit(solution)/shard_map/vmap()/gather
  66.9 0.8 copy_dynamic-update-slice_fusion.2
  67.8 0.6 fusion.47
  68.4 3.3 %dynamic-slice_bitcast_fusion.2 = bf16[1,8,32,3,160]{4,3,2,1,0:T(4,128)(2,1)S(1)} fusion(bf16[40,112,3,192]{3,2,1,0:T(4,128)(2,1)} %get-tuple-element.80, s32[]{:T(128)} %bitcast.20, s32[]{:T(128)} %bitcast.21, s32[]{:T(128)} %bitcast.22), kind=kLoop, calls=%fused_computation.1.clone.1 | loop fusion | bytes 491532 | tf_op jit(solution)/shard_map/vmap()/gather
  71.7 0.8 copy_dynamic-update-slice_fusion.2
  72.6 0.6 fusion.47
  73.2 3.3 %dynamic-slice_bitcast_fusion.2 = bf16[1,8,32,3,160]{4,3,2,1,0:T(4,128)(2,1)S(1)} fusion(bf16[40,112,3,192]{3,2,1,0:T(4,128)(2,1)} %get-tuple-element.80, s32[]{:T(128)} %bitcast.20, s32[]{:T(128)} %bitcast.21, s32[]{:T(128)} %bitcast.22), kind=kLoop, calls=%fused_computation.1.clone.1 | loop fusion | bytes 491532 | tf_op jit(solution)/shard_map/vmap()/gather
  76.5 0.8 copy_dynamic-update-slice_fusion.2
  77.4 0.6 fusion.47
  78.0 3.3 %dynamic-slice_bitcast_fusion.2 = bf16[1,8,32,3,160]{4,3,2,1,0:T(4,128)(2,1)S(1)} fusion(bf16[40,112,3,192]{3,2,1,0:T(4,128)(2,1)} %get-tuple-element.80, s32[]{:T(128)} %bitcast.20, s32[]{:T(128)} %bitcast.21, s32[]{:T(128)} %bitcast.22), kind=kLoop, calls=%fused_computation.1.clone.1 | loop fusion | bytes 491532 | tf_op jit(solution)/shard_map/vmap()/gather
  81.3 0.8 copy_dynamic-update-slice_fusion.2
  82.2 0.6 fusion.47
  82.8 3.3 %dynamic-slice_bitcast_fusion.2 = bf16[1,8,32,3,160]{4,3,2,1,0:T(4,128)(2,1)S(1)} fusion(bf16[40,112,3,192]{3,2,1,0:T(4,128)(2,1)} %get-tuple-element.80, s32[]{:T(128)} %bitcast.20, s32[]{:T(128)} %bitcast.21, s32[]{:T(128)} %bitcast.22), kind=kLoop, calls=%fused_computation.1.clone.1 | loop fusion | bytes 491532 | tf_op jit(solution)/shard_map/vmap()/gather
  86.1 0.8 copy_dynamic-update-slice_fusion.2
  87.0 0.6 fusion.47
  87.6 3.3 %dynamic-slice_bitcast_fusion.2 = bf16[1,8,32,3,160]{4,3,2,1,0:T(4,128)(2,1)S(1)} fusion(bf16[40,112,3,192]{3,2,1,0:T(4,128)(2,1)} %get-tuple-element.80, s32[]{:T(128)} %bitcast.20, s32[]{:T(128)} %bitcast.21, s32[]{:T(128)} %bitcast.22), kind=kLoop, calls=%fused_computation.1.clone.1 | loop fusion | bytes 491532 | tf_op jit(solution)/shard_map/vmap()/gather
  90.9 0.8 copy_dynamic-update-slice_fusion.2
  92.4 3.3 %dynamic-slice_bitcast_fusion.2 = bf16[1,8,32,3,160]{4,3,2,1,0:T(4,128)(2,1)S(1)} fusion(bf16[40,112,3,192]{3,2,1,0:T(4,128)(2,1)} %get-tuple-element.80, s32[]{:T(128)} %bitcast.20, s32[]{:T(128)} %bitcast.21, s32[]{:T(128)} %bitcast.22), kind=kLoop, calls=%fused_computation.1.clone.1 | loop fusion | bytes 491532 | tf_op jit(solution)/shard_map/vmap()/gather
  95.7 0.9 copy_dynamic-update-slice_fusion.2
  97.3 3.3 %dynamic-slice_bitcast_fusion.2 = bf16[1,8,32,3,160]{4,3,2,1,0:T(4,128)(2,1)S(1)} fusion(bf16[40,112,3,192]{3,2,1,0:T(4,128)(2,1)} %get-tuple-element.80, s32[]{:T(128)} %bitcast.20, s32[]{:T(128)} %bitcast.21, s32[]{:T(128)} %bitcast.22), kind=kLoop, calls=%fused_computation.1.clone.1 | loop fusion | bytes 491532 | tf_op jit(solution)/shard_map/vmap()/gather
  100.6 0.8 copy_dynamic-update-slice_fusion.2
  101.4 7.3 %all-to-all-start = ((bf16[16,8,32,3,160]{4,2,3,1,0:T(8,128)(2,1)}), bf16[16,8,32,3,160]{4,2,3,1,0:T(8,128)(2,1)}, u32[]{:S(2)}, u32[]{:S(2)}) async-start(bf16[16,8,32,3,160]{4,2,3,1,0:T(8,128)(2,1)} %get-tuple-element.12), calls=%async_computation | async-start | bytes 12582912 | tf_op jit(solution)/shard_map/all_to_all | solution.py:89
  109.0 0.6 gather_fusion
  110.1 2.3 fusion.1
  112.7 137.1 %all-to-all-done = bf16[16,8,32,3,160]{4,2,3,1,0:T(8,128)(2,1)} async-done(((bf16[16,8,32,3,160]{4,2,3,1,0:T(8,128)(2,1)}), bf16[16,8,32,3,160]{4,2,3,1,0:T(8,128)(2,1)}, u32[]{:S(2)}, u32[]{:S(2)}) %all-to-all-start) | async-done | bytes 3932192 | tf_op jit(solution)/shard_map/all_to_all | solution.py:89
  249.8 6.2 %multiply_reduce_fusion = f32[8,32,3,160]{3,1,2,0:T(8,128)S(1)} fusion(bf16[16,8,32,3,160]{4,2,3,1,0:T(8,128)(2,1)} %all-to-all-done, f32[16,8,32,160]{3,2,1,0:T(8,128)} %get-tuple-element.30), kind=kLoop, calls=%fused_computation.5 | loop fusion | flops 5775360 | bytes 7045120 | tf_op jit(solution)/shard_map/reduce_sum | solution.py:97
  256.5 0.8 fusion.4
  257.3 1.3 collective-permute-start
  258.6 1.3 collective-permute-start.1
  260.1 2.3 collective-permute-done.1
  262.4 0.9 fusion.7
  263.5 0.8 fusion.45
  264.4 0.8 copy.9
  (43 shorter events, 4.5 us)
Async XLA Ops:
  101.4 7.3 %copy-start = (s32[4,4,2,3]{1,2,3,0:T(2,128)S(1)}, s32[4,4,2,3]{1,2,3,0:T(2,128)}, u32[]{:S(2)}) copy-start(s32[4,4,2,3]{1,2,3,0:T(2,128)} %param.4) | copy-start | bytes 1156
  101.4 7.4 %copy-start.1 = (s32[4,4,2]{1,2,0:T(2,128)S(1)}, s32[4,4,2]{1,2,0:T(2,128)}, u32[]{:S(2)}) copy-start(s32[4,4,2]{1,2,0:T(2,128)} %param.5) | copy-start | bytes 388
  101.4 148.4 %all-to-all-start = ((bf16[16,8,32,3,160]{4,2,3,1,0:T(8,128)(2,1)}), bf16[16,8,32,3,160]{4,2,3,1,0:T(8,128)(2,1)}, u32[]{:S(2)}, u32[]{:S(2)}) async-start(bf16[16,8,32,3,160]{4,2,3,1,0:T(8,128)(2,1)} %get-tuple-element.12), calls=%async_computation | async-start | bytes 12582912 | tf_op jit(solution)/shard_map/all_to_all | solution.py:89
  257.3 2.8 %collective-permute-start = (f32[8,32,4,16]{3,2,1,0:T(4,128)S(1)}, f32[8,32,4,16]{3,2,1,0:T(4,128)S(1)}, u32[]{:S(2)}, u32[]{:S(2)}) collective-permute-start(f32[8,32,4,16]{3,2,1,0:T(4,128)S(1)} %get-tuple-element.27), channel_id=1, source_target_pairs={{0,1},{2,3},{4,5},{6,7},{8,9},{10,11},{12,13},{14,15},{16,17},{18,... | collective-permute-start | bytes 196616 | tf_op jit(solution)/shard_map/ppermute | solution.py:23
  258.6 3.8 %collective-permute-start.1 = (f32[8,32,4,16]{3,2,1,0:T(4,128)S(1)}, f32[8,32,4,16]{3,2,1,0:T(4,128)S(1)}, u32[]{:S(2)}, u32[]{:S(2)}) collective-permute-start(f32[8,32,4,16]{3,2,1,0:T(4,128)S(1)} %get-tuple-element.28), channel_id=1, source_target_pairs={{1,0},{3,2},{5,4},{7,6},{9,8},{11,10},{13,12},{15,14},{17,16},{19,... | collective-permute-start | bytes 196616 | tf_op jit(solution)/shard_map/ppermute | solution.py:24
where the time goes:
time: 268 us; the launch traced here: 265 us
  waiting for transfers between devices  140 us (52%)
  local copies, waits for them, and re-layouts  99.4 us (37%)
  other arithmetic  12.7 us (5%)
  starting transfers between devices  9.91 us (4%)
  between operations  3.41 us (1%)
    all_to_all x1, waiting for transfers between devices, per_device(): lax.all_to_all(slot_data, ('gx', 'gy'), split_axis=0, concat_axis=0, tile...  137 us
    gather x64, local copies, waits for them, and re-layouts  76.7 us
    pad x1, local copies, waits for them, and re-layouts, pad_patch(): return jnp.pad(source, ((BX, BX), (BY, BY), (0, 0), (margin, 2 * margin)))  13.3 us
    all_to_all x1, starting transfers between devices, per_device(): lax.all_to_all(slot_data, ('gx', 'gy'), split_axis=0, concat_axis=0, tile...  7.3 us
    reduce_sum x1, other arithmetic, per_device(): canvas = jnp.sum(arrived * weight[:, :, :, None, :], axis=0)  6.15 us
  transfers between devices with their start and end apart: 3, of which 3 were waited for; matrix products, arithmetic and copies ran while one was open for 1% of the time, Pallas kernels for 0%

commit v1 on v0

v1 whole, which is shorter than its diff:
```python
import functools

import jax
import jax.numpy as jnp
from jax import lax
from jax.experimental import pallas as pl
from jax.experimental.pallas import tpu as pltpu
from jax.sharding import PartitionSpec as P

CLASSES = 3
BX = 8
BY = 32
BZ = 128
HALO = 8
PX = 24
PY = 48
PZ = 144
RIM = PZ - BZ
ROWS = CLASSES + 1
GROUP = 8


def profile(offsets, length):
    inside = (offsets >= 0) & (offsets < length)
    centre = (length - 1) / 2.0
    spread = length / 4.0
    values = jnp.exp(-((offsets.astype(jnp.float32) - centre) ** 2) / (2.0 * spread * spread))
    return jnp.where(inside, values, 0.0)


def pack_kernel(lanes_x, place_ref, logits_ref, out_ref):
    start_x = place_ref[0]
    shift_z = place_ref[1]
    rows = lanes_x * BX
    r = lax.broadcasted_iota(jnp.int32, (rows, PX), 0)
    p = lax.broadcasted_iota(jnp.int32, (rows, PX), 1)
    pick = jnp.where(r - start_x == p, 1.0, 0.0).astype(jnp.bfloat16)
    width = GROUP * CLASSES * PZ
    fill = jnp.zeros((rows, 2 * BZ - PZ), jnp.float32)

    def step(g, carry):
        lanes = pl.ds(pl.multiple_of(g * width, 128), width)
        cells = jnp.dot(pick, logits_ref[:, lanes], preferred_element_type=jnp.float32)
        for y in range(GROUP):
            rims = None
            for c in range(CLASSES):
                at = (y * CLASSES + c) * PZ
                line = jnp.concatenate([cells[:, at : at + PZ], fill], axis=1)
                line = pltpu.roll(line, 2 * BZ - shift_z, 1)
                main = line[:, :BZ].astype(jnp.bfloat16)
                rim = pltpu.roll(line[:, BZ:], RIM + 2 * RIM * c, 1)
                rims = rim if rims is None else rims + rim
                for t in range(lanes_x):
                    out_ref[t, g * GROUP + y, c] = main[t * BX : (t + 1) * BX]
            rims = rims.astype(jnp.bfloat16)
            for t in range(lanes_x):
                out_ref[t, g * GROUP + y, CLASSES] = rims[t * BX : (t + 1) * BX]
        return carry

    lax.fori_loop(0, PY // GROUP, step, 0)


def blend_kernel(lanes_x, lanes_y, start_ref, along_y_ref, plane_ref, cells_ref, out_ref):
    def step(row, carry):
        sums = [None] * ROWS
        for p in range(lanes_x):
            q = jnp.clip(row - start_ref[p], 0, PY - 1)
            w = along_y_ref[p, row]
            main = plane_ref[p, 0] * w
            rim = plane_ref[p, 1] * w
            for c in range(ROWS):
                term = cells_ref[p, q, c].astype(jnp.float32) * (main if c < CLASSES else rim)
                sums[c] = term if sums[c] is None else sums[c] + term
        for c in range(ROWS):
            out_ref[row // BY, row % BY, c] = sums[c]
        return carry

    lax.fori_loop(0, lanes_y * BY, step, 0)


def finish_kernel(parts_ref, below_ref, above_ref, weight_ref, out_ref):
    lane = lax.broadcasted_iota(jnp.int32, (BX, BZ), 1)

    def step(y, carry):
        scale = 1.0 / weight_ref[y]
        below = below_ref[y]
        above = above_ref[y]
        scores = []
        for c in range(CLASSES):
            low = pltpu.roll(below, BZ - (2 * RIM * c + RIM), 1)
            high = pltpu.roll(above, BZ - RIM - 2 * RIM * c, 1)
            total = parts_ref[y, c] + jnp.where(lane < RIM, low, 0.0)
            total = total + jnp.where(lane >= BZ - RIM, high, 0.0)
            scores.append(total * scale)
        top = functools.reduce(jnp.maximum, scores)
        powers = [jnp.exp(s - top) for s in scores]
        norm = 1.0 / functools.reduce(jnp.add, powers)
        for c in range(CLASSES):
            out_ref[y, c] = powers[c] * norm
        return carry

    lax.fori_loop(0, BY, step, 0)


VMEM = pl.BlockSpec(memory_space=pltpu.VMEM)
SMEM = pl.BlockSpec(memory_space=pltpu.SMEM)


def per_device(patch_logits, patch_start, patch_owner):
    lanes_x = lax.axis_size("gx")
    lanes_y = lax.axis_size("gy")
    lanes_z = lax.axis_size("gz")
    place_x = lax.axis_index("gx")
    place_y = lax.axis_index("gy")
    place_z = lax.axis_index("gz")
    cells_y = lanes_y * BY
    codes = patch_owner[:, place_y, place_z]
    corners = patch_start[codes // lanes_y, codes % lanes_y, place_z]
    corner = corners[place_x]
    place = jnp.stack([corner[0], place_z * BZ - corner[2]])
    packed = pl.pallas_call(
        functools.partial(pack_kernel, lanes_x),
        out_shape=jax.ShapeDtypeStruct((lanes_x, PY, ROWS, BX, BZ), jnp.bfloat16),
        in_specs=[SMEM, VMEM],
        out_specs=VMEM,
    )(place, patch_logits[0, 0, 0])
    arrived = lax.all_to_all(packed, "gx", split_axis=0, concat_axis=0, tiled=True)

    along_x = profile(place_x * BX + jnp.arange(BX)[None, :] - corners[:, 0:1], PX)
    along_y = profile(jnp.arange(cells_y)[None, :] - corners[:, 1:2], PY)
    shift = place_z * BZ - corners[:, 2:3]
    main_z = profile(jnp.arange(BZ)[None, :] + shift, PZ)
    j = jnp.arange(RIM)[None, :]
    rim_z = jnp.concatenate([profile(j + shift - RIM, PZ), profile(BZ + j + shift, PZ)], axis=1)
    rim_z = jnp.pad(jnp.tile(rim_z, (1, CLASSES)), ((0, 0), (0, BZ - 2 * RIM * CLASSES)))
    plane = along_x[:, None, :, None] * jnp.stack([main_z, rim_z], axis=1)[:, :, None, :]
    parts = pl.pallas_call(
        functools.partial(blend_kernel, lanes_x, lanes_y),
        out_shape=jax.ShapeDtypeStruct((lanes_y, BY, ROWS, BX, BZ), jnp.float32),
        in_specs=[SMEM, SMEM, VMEM, VMEM],
        out_specs=VMEM,
    )(corners[:, 1], along_y, plane, arrived)
    parts = lax.all_to_all(parts, "gy", split_axis=0, concat_axis=0, tiled=True)
    parts = jnp.sum(parts, axis=0)

    layers = jnp.clip(place_z + jnp.arange(-1, 2), 0, lanes_z - 1)
    real = (place_z + jnp.arange(-1, 2) >= 0) & (place_z + jnp.arange(-1, 2) < lanes_z)
    near = jnp.take(patch_start, layers, axis=2)
    every_x = profile(place_x * BX + jnp.arange(BX) - near[..., 0:1], PX)
    every_y = profile(place_y * BY + jnp.arange(BY) - near[..., 1:2], PY)
    every_z = profile(place_z * BZ + jnp.arange(BZ) - near[..., 2:3], PZ)
    every_z = jnp.where(real[None, None, :, None], every_z, 0.0)
    every_y = every_y.reshape(-1, BY)
    every_xz = (every_x[..., :, None] * every_z[..., None, :]).reshape(-1, BX * BZ)
    weight = lax.dot_general(
        every_y, every_xz, (((0,), (0,)), ((), ())), precision=lax.Precision.HIGHEST
    ).reshape(BY, BX, BZ)

    rims = parts[:, CLASSES]
    up = [(i, i + 1) for i in range(lanes_z - 1)]
    down = [(j, i) for i, j in up]
    below = lax.ppermute(rims, "gz", up)
    above = lax.ppermute(rims, "gz", down)
    probs = pl.pallas_call(
        finish_kernel,
        out_shape=jax.ShapeDtypeStruct((BY, CLASSES, BX, BZ), jnp.float32),
        in_specs=[VMEM] * 4,
        out_specs=VMEM,
    )(parts, below, above, weight)
    return jnp.transpose(probs, (2, 0, 1, 3))


def solution(mesh):
    return jax.shard_map(
        per_device,
        mesh=mesh,
        in_specs=(P("gx", "gy", "gz", None, None), P(), P()),
        out_specs=P("gx", "gy", None, "gz"),
        check_vma=False,
    )
```

time: 268 us -> 106 us (0.40)
  the two profiles are of different devices: /device:TPU:12 before, /device:TPU:1 now
where the time goes in v1:
time: 106 us
  waiting for transfers between devices  57.3 us (54%)
  Pallas kernels  21.1 us (20%)
  starting transfers between devices  13.8 us (13%)
  local copies, waits for them, and re-layouts  8.46 us (8%)
  other arithmetic  3.78 us (4%)
    all_to_all x1, waiting for transfers between devices, per_device(): lax.all_to_all(packed, 'gx', split_axis=0, concat_axis=0, tiled=True)  34.5 us
    all_to_all x1, waiting for transfers between devices, per_device(): parts = lax.all_to_all(parts, 'gy', split_axis=0, concat_axis=0, tiled=True)  22.8 us
    pallas_call x1, Pallas kernels, per_device(): pl.pallas_call(functools.partial(pack_kernel, lanes_x), out_shape=jax.Sha...  10.4 us
    pallas_call x1, Pallas kernels, per_device(): pl.pallas_call(functools.partial(blend_kernel, lanes_x, lanes_y), out_sha...  5.73 us
    all_to_all x1, starting transfers between devices, per_device(): lax.all_to_all(packed, 'gx', split_axis=0, concat_axis=0, tiled=True)  5.41 us
    pallas_call x1, Pallas kernels, per_device(): pl.pallas_call(finish_kernel, out_shape=jax.ShapeDtypeStruct((BY, CLASSES...  4.98 us
    all_to_all x1, starting transfers between devices, per_device(): parts = lax.all_to_all(parts, 'gy', split_axis=0, concat_axis=0, tiled=True)  3.74 us
    ppermute x1, starting transfers between devices, per_device(): above = lax.ppermute(rims, 'gz', down)  3.36 us
  transfers between devices with their start and end apart: 4, of which 2 were waited for; matrix products, arithmetic and copies ran while one was open for 4% of the time, Pallas kernels for 0%

profile of v1, /device:TPU:1, one launch (start us, length us, event | category | flops | bytes accessed | tf_op | source)
XLA Modules:
  0.0 105.6 jit_solution(11274214715816273208)
XLA Ops:
  0.0 0.0 copy-start
  0.0 0.8 copy.24
  0.9 0.0 copy-done
  0.9 0.2 dynamic-slice_reduce_fusion
  1.1 0.6 gather_fusion
  1.7 0.6 fusion.70
  3.0 1.2 %pad_add_fusion.place_ref = s32[2]{0:T(128)} fusion(s32[1]{0:T(128)} %bitcast.4, s32[1]{0:T(128)} %bitcast.2), kind=kLoop, calls=%fused_computation.111 | loop fusion | flops 2 | bytes 16 | tf_op jit(solution)/shard_map/stack | solution.py:120
  4.2 10.4 %shard_map.37 = bf16[4,48,4,8,128]{4,3,2,1,0:T(8,128)(2,1)} custom-call(s32[2]{0:T(128)} %pad_add_fusion.place_ref, bf16[24,20736]{1,0:T(8,128)(2,1)} %bitcast.56), custom_call_target="tpu_custom_call" | custom-call | tf_op jit(solution)/shard_map/pallas_call | solution.py:121
  14.5 5.4 %all-to-all-start = ((bf16[4,48,4,8,128]{4,3,2,1,0:T(8,128)(2,1)}), bf16[4,48,4,8,128]{4,3,2,1,0:T(8,128)(2,1)S(1)}, u32[]{:S(2)}, u32[]{:S(2)}) async-start(bf16[4,48,4,8,128]{4,3,2,1,0:T(8,128)(2,1)} %shard_map.37), calls=%async_computation | async-start | bytes 3145728 | tf_op jit(solution)/shard_map/all_to_all | solution.py:127
  19.9 0.2 slice_reduce_fusion
  20.1 0.0 copy-start.6
  20.1 0.1 exponential_select_fusion
  20.2 0.1 pad_maximum_fusion.1
  20.3 0.1 tile.10
  20.4 0.1 exponential_select_fusion.1
  20.5 0.7 exponential_select_fusion.2.along_y_ref
  21.2 0.1 fusion.40
  21.3 0.7 broadcast_multiply_fusion.1.plane_ref
  22.0 34.5 %all-to-all-done.cells_ref = bf16[4,48,4,8,128]{4,3,2,1,0:T(8,128)(2,1)S(1)} async-done(((bf16[4,48,4,8,128]{4,3,2,1,0:T(8,128)(2,1)}), bf16[4,48,4,8,128]{4,3,2,1,0:T(8,128)(2,1)S(1)}, u32[]{:S(2)}, u32[]{:S(2)}) %all-to-all-start) | async-done | bytes 1572896 | tf_op jit(solution)/shard_map/all_to_all | solution.py:127
  56.5 0.0 copy-done.6
  56.5 0.0 copy-start.1
  56.5 1.1 %copy-done.1 = bf16[4,48,4,8,128]{4,3,2,1,0:T(8,128)(2,1)} copy-done((bf16[4,48,4,8,128]{4,3,2,1,0:T(8,128)(2,1)}, bf16[4,48,4,8,128]{4,3,2,1,0:T(8,128)(2,1)S(1)}, u32[]{:S(2)}) %copy-start.1) | copy-done | bytes 1572888
  57.6 5.7 %shard_map.38 = f32[4,32,4,8,128]{4,3,2,1,0:T(8,128)} custom-call(s32[4]{0:T(128)} %copy-done.6, f32[4,128]{1,0:T(4,128)} %exponential_select_fusion.2.along_y_ref, f32[4,2,8,128]{3,2,1,0:T(8,128)} %broadcast_multiply_fusion.1.plane_ref, bf16[4,48,4,8,128]{4,3,2,1,0:T(8,128)(2,1)} %copy-done.1), custom_call_target="tpu_custom_call" | custom-call | tf_op jit(solution)/shard_map/pallas_call | solution.py:137
  63.4 0.0 copy-start.2
  63.4 3.7 %all-to-all-start.1 = ((f32[4,32,4,8,128]{4,3,2,1,0:T(8,128)}), f32[4,32,4,8,128]{4,3,2,1,0:T(8,128)S(1)}, u32[]{:S(2)}, u32[]{:S(2)}) async-start(f32[4,32,4,8,128]{4,3,2,1,0:T(8,128)} %shard_map.38), calls=%async_computation.1 | async-start | bytes 4194304 | tf_op jit(solution)/shard_map/all_to_all | solution.py:143
  67.1 0.0 copy-done.2
  67.1 0.6 gather_fusion.1
  67.8 0.1 select_bitcast_fusion
  67.8 0.1 copy.31
  68.0 0.1 copy.29
  68.1 0.1 copy.27
  68.2 0.1 sub.157
  68.3 0.1 fusion.8
  68.4 0.1 fusion.15
  68.5 0.1 broadcast_multiply_fusion
  68.6 22.8 %all-to-all-done.1 = f32[4,32,4,8,128]{4,3,2,1,0:T(8,128)S(1)} async-done(((f32[4,32,4,8,128]{4,3,2,1,0:T(8,128)}), f32[4,32,4,8,128]{4,3,2,1,0:T(8,128)S(1)}, u32[]{:S(2)}, u32[]{:S(2)}) %all-to-all-start.1) | async-done | bytes 2097184 | tf_op jit(solution)/shard_map/all_to_all | solution.py:143
  91.4 0.3 reduce_sum.9.parts_ref
  91.7 0.0 copy-start.3
  91.7 1.3 %collective-permute-start = (f32[32,8,128]{2,1,0:T(8,128)S(1)}, f32[32,8,128]{2,1,0:T(8,128)S(1)}, u32[]{:S(2)}, u32[]{:S(2)}) collective-permute-start(f32[32,8,128]{2,1,0:T(8,128)S(1)} %slice_bitcast_fusion), channel_id=1, source_target_pairs={{0,1},{2,3},{4,5},{6,7},{8,9},{10,11},{12,13},{14,15},{16,17},{18,... | collective-permute-start | bytes 393224 | tf_op jit(solution)/shard_map/ppermute | solution.py:162
  93.0 3.4 %collective-permute-start.1 = (f32[32,8,128]{2,1,0:T(8,128)S(1)}, f32[32,8,128]{2,1,0:T(8,128)S(1)}, u32[]{:S(2)}, u32[]{:S(2)}) collective-permute-start(f32[32,8,128]{2,1,0:T(8,128)S(1)} %slice_bitcast_fusion), channel_id=1, source_target_pairs={{1,0},{3,2},{5,4},{7,6},{9,8},{11,10},{13,12},{15,14},{17,16},{19,... | collective-permute-start | bytes 393224 | tf_op jit(solution)/shard_map/ppermute | solution.py:163
  96.4 0.3 fusion
  96.7 0.7 copy.33.weight_ref
  97.5 0.0 collective-permute-done.below_ref
  97.5 0.0 copy-start.4
  97.5 0.0 collective-permute-done.1.above_ref
  97.5 0.0 copy-done.3
  97.5 0.6 copy-done.4
  98.1 0.0 copy-start.5
  98.1 0.7 copy-done.5
  98.8 5.0 %shard_map.39 = f32[32,3,8,128]{3,2,1,0:T(8,128)} custom-call(f32[32,4,8,128]{3,2,1,0:T(8,128)} %copy-done.3, f32[32,8,128]{2,1,0:T(8,128)} %copy-done.4, f32[32,8,128]{2,1,0:T(8,128)} %copy-done.5, f32[32,8,128]{2,1,0:T(8,128)} %copy.33.weight_ref), custom_call_target="tpu_custom_call" | custom-call | tf_op jit(solution)/shard_map/pallas_call | solution.py:164
  103.8 1.8 %copy.34 = f32[8,32,3,128]{3,1,2,0:T(8,128)} copy(f32[8,32,3,128]{3,0,2,1:T(8,128)} %bitcast.55) | data formatting | bytes 786432 | tf_op jit(solution)/shard_map/transpose | solution.py:170
  (15 shorter events, 0.1 us)
Async XLA Ops:
  0.0 0.9 copy-start
  14.5 41.9 %all-to-all-start = ((bf16[4,48,4,8,128]{4,3,2,1,0:T(8,128)(2,1)}), bf16[4,48,4,8,128]{4,3,2,1,0:T(8,128)(2,1)S(1)}, u32[]{:S(2)}, u32[]{:S(2)}) async-start(bf16[4,48,4,8,128]{4,3,2,1,0:T(8,128)(2,1)} %shard_map.37), calls=%async_computation | async-start | bytes 3145728 | tf_op jit(solution)/shard_map/all_to_all | solution.py:127
  20.1 36.3 %copy-start.6 = (s32[4]{0:T(128)}, s32[4]{0:T(128)S(1)}, u32[]{:S(2)}) copy-start(s32[4]{0:T(128)S(1)} %get-tuple-element.7.start_ref) | copy-start | bytes 52
  56.5 1.1 %copy-start.1 = (bf16[4,48,4,8,128]{4,3,2,1,0:T(8,128)(2,1)}, bf16[4,48,4,8,128]{4,3,2,1,0:T(8,128)(2,1)S(1)}, u32[]{:S(2)}) copy-start(bf16[4,48,4,8,128]{4,3,2,1,0:T(8,128)(2,1)S(1)} %all-to-all-done.cells_ref) | copy-start | bytes 4718596
  63.4 3.8 %copy-start.2 = (s32[4,4,2,3]{1,2,3,0:T(2,128)S(1)}, s32[4,4,2,3]{1,2,3,0:T(2,128)}, u32[]{:S(2)}) copy-start(s32[4,4,2,3]{1,2,3,0:T(2,128)} %param.4) | copy-start | bytes 1156
  63.4 28.1 %all-to-all-start.1 = ((f32[4,32,4,8,128]{4,3,2,1,0:T(8,128)}), f32[4,32,4,8,128]{4,3,2,1,0:T(8,128)S(1)}, u32[]{:S(2)}, u32[]{:S(2)}) async-start(f32[4,32,4,8,128]{4,3,2,1,0:T(8,128)} %shard_map.38), calls=%async_computation.1 | async-start | bytes 4194304 | tf_op jit(solution)/shard_map/all_to_all | solution.py:143
  91.7 5.8 %copy-start.3 = (f32[32,4,8,128]{3,2,1,0:T(8,128)}, f32[32,4,8,128]{3,2,1,0:T(8,128)S(1)}, u32[]{:S(2)}) copy-start(f32[32,4,8,128]{3,2,1,0:T(8,128)S(1)} %reduce_sum.9.parts_ref) | copy-start | bytes 1572868
  91.7 5.7 %collective-permute-start = (f32[32,8,128]{2,1,0:T(8,128)S(1)}, f32[32,8,128]{2,1,0:T(8,128)S(1)}, u32[]{:S(2)}, u32[]{:S(2)}) collective-permute-start(f32[32,8,128]{2,1,0:T(8,128)S(1)} %slice_bitcast_fusion), channel_id=1, source_target_pairs={{0,1},{2,3},{4,5},{6,7},{8,9},{10,11},{12,13},{14,15},{16,17},{18,... | collective-permute-start | bytes 393224 | tf_op jit(solution)/shard_map/ppermute | solution.py:162
  93.0 4.4 %collective-permute-start.1 = (f32[32,8,128]{2,1,0:T(8,128)S(1)}, f32[32,8,128]{2,1,0:T(8,128)S(1)}, u32[]{:S(2)}, u32[]{:S(2)}) collective-permute-start(f32[32,8,128]{2,1,0:T(8,128)S(1)} %slice_bitcast_fusion), channel_id=1, source_target_pairs={{1,0},{3,2},{5,4},{7,6},{9,8},{11,10},{13,12},{15,14},{17,16},{19,... | collective-permute-start | bytes 393224 | tf_op jit(solution)/shard_map/ppermute | solution.py:163
  97.5 0.7 copy-start.4
  98.1 0.7 copy-start.5

commit v2 on v1

v2 whole, which is shorter than its diff:
```python
import functools

import jax
import jax.numpy as jnp
from jax import lax
from jax.experimental import pallas as pl
from jax.experimental.pallas import tpu as pltpu
from jax.sharding import PartitionSpec as P

CLASSES = 3
BX = 8
BY = 32
BZ = 128
HALO = 8
PX = 24
PY = 48
PZ = 144
RIM = PZ - BZ
ROWS = CLASSES + 1
GROUP = 8
MESH = pl.DeviceIdType.MESH


def profile(offsets, length):
    inside = (offsets >= 0) & (offsets < length)
    centre = (length - 1) / 2.0
    spread = length / 4.0
    values = jnp.exp(-((offsets.astype(jnp.float32) - centre) ** 2) / (2.0 * spread * spread))
    return jnp.where(inside, values, 0.0)


def pack_kernel(lanes_x, place_ref, logits_ref, out_ref):
    start_x = place_ref[0]
    shift_z = place_ref[1]
    place_x = place_ref[2]
    rows = lanes_x * BX
    r = lax.broadcasted_iota(jnp.int32, (rows, PX), 0)
    p = lax.broadcasted_iota(jnp.int32, (rows, PX), 1)
    x = r + place_x * BX
    x = jnp.where(x >= rows, x - rows, x)
    pick = jnp.where(x - start_x == p, 1.0, 0.0).astype(jnp.bfloat16)
    width = GROUP * CLASSES * PZ
    fill = jnp.zeros((rows, 2 * BZ - PZ), jnp.float32)

    def step(g, carry):
        lanes = pl.ds(pl.multiple_of(g * width, 128), width)
        cells = jnp.dot(pick, logits_ref[:, lanes], preferred_element_type=jnp.float32)
        for y in range(GROUP):
            rims = None
            for c in range(CLASSES):
                at = (y * CLASSES + c) * PZ
                line = jnp.concatenate([cells[:, at : at + PZ], fill], axis=1)
                line = pltpu.roll(line, 2 * BZ - shift_z, 1)
                main = line[:, :BZ].astype(jnp.bfloat16)
                rim = pltpu.roll(line[:, BZ:], RIM + 2 * RIM * c, 1)
                rims = rim if rims is None else rims + rim
                for t in range(lanes_x):
                    out_ref[c, t, g * GROUP + y] = main[t * BX : (t + 1) * BX]
            rims = rims.astype(jnp.bfloat16)
            for t in range(lanes_x):
                out_ref[CLASSES, t, g * GROUP + y] = rims[t * BX : (t + 1) * BX]
        return carry

    lax.fori_loop(0, PY // GROUP, step, 0)


def blend_kernel(
    lanes_x, lanes_y, lanes_z,
    start_ref, along_y_ref, plane_ref, weight_ref, packed_ref, out_ref,
    land0, land1, land2, land3, parts, parts_land, rims, rims_land,
    cells_out, cells_in, parts_out, parts_in, rims_out, rims_in,
):
    place_x = lax.axis_index("gx")
    place_y = lax.axis_index("gy")
    place_z = lax.axis_index("gz")

    cells_land = (land0, land1, land2, land3)

    def ahead(place, d, size):
        return lax.rem(place + d, size)

    barrier = pltpu.get_barrier_semaphore()
    peers = [{"gx": ahead(place_x, d, lanes_x)} for d in range(1, lanes_x)]
    peers += [{"gy": ahead(place_y, d, lanes_y)} for d in range(1, lanes_y)]
    peers += [{"gz": ahead(place_z, d, lanes_z)} for d in (1, lanes_z - 1)]
    for peer in peers:
        pl.semaphore_signal(barrier, inc=1, device_id=peer, device_id_type=MESH)
    pl.semaphore_wait(barrier, len(peers))

    order = (CLASSES,) + tuple(range(CLASSES))
    far_x = sorted(range(1, lanes_x), key=lambda d: -min(d, lanes_x - d))
    far_y = sorted(range(1, lanes_y), key=lambda d: -min(d, lanes_y - d))
    cell_copies = {
        (c, d): pltpu.make_async_remote_copy(
            src_ref=packed_ref.at[c, d],
            dst_ref=cells_land[c].at[d],
            send_sem=cells_out.at[c, d],
            recv_sem=cells_in.at[c, d],
            device_id={"gx": ahead(place_x, d, lanes_x)},
            device_id_type=MESH,
        )
        for c in order
        for d in far_x
    }
    part_copies = {
        (c, d): pltpu.make_async_remote_copy(
            src_ref=parts.at[c, d],
            dst_ref=parts_land.at[c, d],
            send_sem=parts_out.at[c, d],
            recv_sem=parts_in.at[c, d],
            device_id={"gy": ahead(place_y, d, lanes_y)},
            device_id_type=MESH,
        )
        for c in order
        for d in far_y
    }
    rim_copies = [
        pltpu.make_async_remote_copy(
            src_ref=rims,
            dst_ref=rims_land.at[side],
            send_sem=rims_out.at[side],
            recv_sem=rims_in.at[side],
            device_id={"gz": ahead(place_z, d, lanes_z)},
            device_id_type=MESH,
        )
        for side, d in ((0, 1), (1, lanes_z - 1))
    ]
    for c in order:
        for d in far_x:
            cell_copies[c, d].start()

    def blend(c):
        kind = 0 if c < CLASSES else 1
        for d in far_y + [0]:
            base = ahead(place_y, d, lanes_y) * BY

            def step(y, carry):
                row = base + y
                total = None
                for p in range(lanes_x):
                    q = jnp.clip(row - start_ref[p], 0, PY - 1)
                    cells = packed_ref[c, 0, q] if p == 0 else cells_land[c][p, q]
                    term = cells.astype(jnp.float32) * (plane_ref[p, kind] * along_y_ref[p, row])
                    total = term if total is None else total + term
                parts[c, d, y] = total
                return carry

            lax.fori_loop(0, BY, step, 0, unroll=2)
            if d:
                part_copies[c, d].start()

    def gathered(c, y):
        total = parts[c, 0, y]
        for d in range(1, lanes_y):
            total = total + parts_land[c, d, y]
        return total

    for c in order:
        for d in far_x:
            cell_copies[c, d].wait_recv()
        blend(c)
        if c == 0:
            for d in far_y:
                part_copies[CLASSES, d].wait_recv()

            def add_rims(y, carry):
                rims[y] = gathered(CLASSES, y)
                return carry

            lax.fori_loop(0, BY, add_rims, 0)
            for copy in rim_copies:
                copy.start()

    for copy in rim_copies:
        copy.wait_recv()
    for c in range(CLASSES):
        for d in far_y:
            part_copies[c, d].wait_recv()

    lane = lax.broadcasted_iota(jnp.int32, (BX, BZ), 1)
    low_lanes = (lane < RIM) & (place_z > 0)
    high_lanes = (lane >= BZ - RIM) & (place_z < lanes_z - 1)

    def finish(y, carry):
        scale = 1.0 / weight_ref[y]
        below = rims_land[0, y]
        above = rims_land[1, y]
        scores = []
        for c in range(CLASSES):
            low = pltpu.roll(below, BZ - (2 * RIM * c + RIM), 1)
            high = pltpu.roll(above, BZ - RIM - 2 * RIM * c, 1)
            total = gathered(c, y) + jnp.where(low_lanes, low, 0.0)
            total = total + jnp.where(high_lanes, high, 0.0)
            scores.append(total * scale)
        top = functools.reduce(jnp.maximum, scores)
        powers = [jnp.exp(s - top) for s in scores]
        norm = 1.0 / functools.reduce(jnp.add, powers)
        for c in range(CLASSES):
            out_ref[y, c] = powers[c] * norm
        return carry

    lax.fori_loop(0, BY, finish, 0, unroll=2)
    for copy in list(cell_copies.values()) + list(part_copies.values()) + rim_copies:
        copy.wait_send()


VMEM = pl.BlockSpec(memory_space=pltpu.VMEM)
SMEM = pl.BlockSpec(memory_space=pltpu.SMEM)


def per_device(patch_logits, patch_start, patch_owner):
    lanes_x = lax.axis_size("gx")
    lanes_y = lax.axis_size("gy")
    lanes_z = lax.axis_size("gz")
    place_x = lax.axis_index("gx")
    place_y = lax.axis_index("gy")
    place_z = lax.axis_index("gz")
    cells_y = lanes_y * BY
    behind = lax.rem(place_x - jnp.arange(lanes_x) + lanes_x, lanes_x)
    codes = patch_owner[behind, place_y, place_z]
    corners = patch_start[codes // lanes_y, codes % lanes_y, place_z]
    place = jnp.stack([corners[0, 0], place_z * BZ - corners[0, 2], place_x])
    packed = pl.pallas_call(
        functools.partial(pack_kernel, lanes_x),
        out_shape=jax.ShapeDtypeStruct((ROWS, lanes_x, PY, BX, BZ), jnp.bfloat16),
        in_specs=[SMEM, VMEM],
        out_specs=VMEM,
    )(place, patch_logits[0, 0, 0])

    along_x = profile(place_x * BX + jnp.arange(BX)[None, :] - corners[:, 0:1], PX)
    along_y = profile(jnp.arange(cells_y)[None, :] - corners[:, 1:2], PY)
    shift = place_z * BZ - corners[:, 2:3]
    main_z = profile(jnp.arange(BZ)[None, :] + shift, PZ)
    j = jnp.arange(RIM)[None, :]
    rim_z = jnp.concatenate([profile(j + shift - RIM, PZ), profile(BZ + j + shift, PZ)], axis=1)
    rim_z = jnp.pad(jnp.tile(rim_z, (1, CLASSES)), ((0, 0), (0, BZ - 2 * RIM * CLASSES)))
    plane = along_x[:, None, :, None] * jnp.stack([main_z, rim_z], axis=1)[:, :, None, :]

    layers = jnp.clip(place_z + jnp.arange(-1, 2), 0, lanes_z - 1)
    real = (place_z + jnp.arange(-1, 2) >= 0) & (place_z + jnp.arange(-1, 2) < lanes_z)
    near = jnp.take(patch_start, layers, axis=2)
    every_x = profile(place_x * BX + jnp.arange(BX) - near[..., 0:1], PX)
    every_y = profile(place_y * BY + jnp.arange(BY) - near[..., 1:2], PY)
    every_z = profile(place_z * BZ + jnp.arange(BZ) - near[..., 2:3], PZ)
    every_z = jnp.where(real[None, None, :, None], every_z, 0.0)
    every_y = every_y.reshape(-1, BY)
    every_xz = (every_x[..., :, None] * every_z[..., None, :]).reshape(-1, BX * BZ)
    weight = lax.dot_general(
        every_y, every_xz, (((0,), (0,)), ((), ())), precision=lax.Precision.HIGHEST
    ).reshape(BY, BX, BZ)

    cells_shape = (lanes_x, PY, BX, BZ)
    parts_shape = (ROWS, lanes_y, BY, BX, BZ)
    probs = pl.pallas_call(
        functools.partial(blend_kernel, lanes_x, lanes_y, lanes_z),
        out_shape=jax.ShapeDtypeStruct((BY, CLASSES, BX, BZ), jnp.float32),
        in_specs=[SMEM, SMEM, VMEM, VMEM, VMEM],
        out_specs=VMEM,
        scratch_shapes=[
            *[pltpu.VMEM(cells_shape, jnp.bfloat16)] * ROWS,
            pltpu.VMEM(parts_shape, jnp.float32),
            pltpu.VMEM(parts_shape, jnp.float32),
            pltpu.VMEM((BY, BX, BZ), jnp.float32),
            pltpu.VMEM((2, BY, BX, BZ), jnp.float32),
            pltpu.SemaphoreType.DMA((ROWS, lanes_x)),
            pltpu.SemaphoreType.DMA((ROWS, lanes_x)),
            pltpu.SemaphoreType.DMA((ROWS, lanes_y)),
            pltpu.SemaphoreType.DMA((ROWS, lanes_y)),
            pltpu.SemaphoreType.DMA((2,)),
            pltpu.SemaphoreType.DMA((2,)),
        ],
        compiler_params=pltpu.CompilerParams(collective_id=0, has_side_effects=True),
    )(corners[:, 1], along_y, plane, weight, packed)
    return jnp.transpose(probs, (2, 0, 1, 3))


def solution(mesh):
    return jax.shard_map(
        per_device,
        mesh=mesh,
        in_specs=(P("gx", "gy", "gz", None, None), P(), P()),
        out_specs=P("gx", "gy", None, "gz"),
        check_vma=False,
    )
```

time: 106 us -> 76.4 us (0.72)
  the two profiles are of different devices: /device:TPU:1 before, /device:TPU:12 now
where the time goes in v2:
time: 76.4 us; the launch traced here: 76.1 us
  Pallas kernels  63.6 us (83%)
  local copies, waits for them, and re-layouts  7.76 us (10%)
  other arithmetic  3.62 us (5%)
    pallas_call x1, Pallas kernels, per_device(): pl.pallas_call(functools.partial(blend_kernel, lanes_x, lanes_y, lanes_z)...  53.3 us
    pallas_call x1, Pallas kernels, per_device(): pl.pallas_call(functools.partial(pack_kernel, lanes_x), out_shape=jax.Sha...  10.4 us
    transpose x1, local copies, waits for them, and re-layouts, per_device(): return jnp.transpose(probs, (2, 0, 1, 3))  1.82 us

profile of v2, /device:TPU:12, one launch (start us, length us, event | category | flops | bytes accessed | tf_op | source)
XLA Modules:
  0.0 76.1 jit_solution(8637174571549141031)
XLA Ops:
  0.0 0.0 copy-start
  0.0 0.6 copy-done
  0.7 0.6 gather_fusion
  1.4 0.8 %copy.12 = s32[4,4,2,3]{3,2,1,0:T(2,128)S(1)} copy(s32[4,4,2,3]{1,2,3,0:T(2,128)} %param.4) | data formatting | bytes 768 | tf_op args[1]
  2.3 0.6 gather_fusion.1
  2.9 0.6 fusion.76
  4.1 1.3 %pad_add_fusion.place_ref = s32[3]{0:T(128)} fusion(s32[1]{0:T(128)} %bitcast.13, s32[1]{0:T(128)} %bitcast.12, s32[1]{0:T(128)} %bitcast.10), kind=kLoop, calls=%fused_computation.119 | loop fusion | flops 6 | bytes 24 | tf_op jit(solution)/shard_map/stack | solution.py:222
  5.4 0.2 slice_reduce_fusion
  5.6 0.0 copy-start.1
  5.6 0.1 fusion.40
  5.7 0.1 exponential_select_fusion.1
  5.8 0.7 exponential_select_fusion.2.along_y_ref
  6.4 0.1 exponential_select_fusion
  6.5 0.1 pad_maximum_fusion.1
  6.6 0.1 tile.10
  6.7 1.3 %gather_fusion.2 = s32[3,4,4,3]{2,0,3,1:T(4,128)S(1)} fusion(s32[4,4,2,3]{1,2,3,0:T(2,128)} %param.4, s32[1024]{0:T(1024)S(1)} %pad_clamp_fusion), kind=kCustom, calls=%fused_computation.2 | custom fusion | bytes 1164 | tf_op jit(solution)/shard_map/jit(_take)/gather | solution.py:241
  8.0 0.1 select_bitcast_fusion
  8.1 0.1 copy.14
  8.2 0.1 sub.171
  8.3 0.1 copy.18
  8.4 0.1 copy.16
  8.6 0.1 fusion.15
  8.7 0.1 fusion.8
  8.8 0.7 broadcast_multiply_fusion.1.plane_ref
  9.4 0.1 broadcast_multiply_fusion
  9.6 0.3 fusion
  9.9 0.7 copy.20.weight_ref
  10.6 10.4 %shard_map.37.packed_ref = bf16[4,4,48,8,128]{4,3,2,1,0:T(8,128)(2,1)} custom-call(s32[3]{0:T(128)} %pad_add_fusion.place_ref, bf16[24,20736]{1,0:T(8,128)(2,1)} %bitcast.55), custom_call_target="tpu_custom_call" | custom-call | tf_op jit(solution)/shard_map/pallas_call | solution.py:223
  21.0 0.0 copy-done.1
  21.0 53.3 %shard_map.38 = f32[32,3,8,128]{3,2,1,0:T(8,128)} custom-call(s32[4]{0:T(128)} %copy-done.1, f32[4,128]{1,0:T(4,128)} %exponential_select_fusion.2.along_y_ref, f32[4,2,8,128]{3,2,1,0:T(8,128)} %broadcast_multiply_fusion.1.plane_ref, f32[32,8,128]{2,1,0:T(8,128)} %copy.20.weight_ref, bf16[4,4,48,8,128]{4,3,2,1,0:T(8,128)(2,1)} %shard_map.37.packed_ref), custom_call_target="tpu_custom_call" | custom-call | tf_op jit(solution)/shard_map/pallas_call | solution.py:254
  74.3 1.8 %copy.21 = f32[8,32,3,128]{3,1,2,0:T(8,128)} copy(f32[8,32,3,128]{3,0,2,1:T(8,128)} %bitcast.54) | data formatting | bytes 786432 | tf_op jit(solution)/shard_map/transpose | solution.py:274
  (14 shorter events, 0.1 us)
Async XLA Ops:
  0.0 0.7 copy-start
  5.6 15.4 %copy-start.1 = (s32[4]{0:T(128)}, s32[4]{0:T(128)S(1)}, u32[]{:S(2)}) copy-start(s32[4]{0:T(128)S(1)} %get-tuple-element.7.start_ref) | copy-start | bytes 52

commit v3 on v2

--- a/solution.py
+++ b/solution.py
@@ -21,18 +21,24 @@
 MESH = pl.DeviceIdType.MESH
 
 
-def profile(offsets, length):
-    inside = (offsets >= 0) & (offsets < length)
+def profile(offsets, length, keep=True):
+    inside = (offsets >= 0) & (offsets < length) & keep
     centre = (length - 1) / 2.0
     spread = length / 4.0
-    values = jnp.exp(-((offsets.astype(jnp.float32) - centre) ** 2) / (2.0 * spread * spread))
+    values = jnp.exp((offsets.astype(jnp.float32) - centre) ** 2 * (-0.5 / (spread * spread)))
     return jnp.where(inside, values, 0.0)
 
 
-def pack_kernel(lanes_x, place_ref, logits_ref, out_ref):
-    start_x = place_ref[0]
-    shift_z = place_ref[1]
-    place_x = place_ref[2]
+def corner_of(start_ref, code, lanes_y, layer):
+    return [start_ref[code // lanes_y, code % lanes_y, layer, k] for k in range(3)]
+
+
+def pack_kernel(lanes_x, lanes_y, start_ref, owner_ref, logits_ref, out_ref):
+    place_x = lax.axis_index("gx")
+    place_z = lax.axis_index("gz")
+    code = owner_ref[place_x, lax.axis_index("gy"), place_z]
+    start_x, _, start_z = corner_of(start_ref, code, lanes_y, place_z)
+    shift_z = place_z * BZ - start_z
     rows = lanes_x * BX
     r = lax.broadcasted_iota(jnp.int32, (rows, PX), 0)
     p = lax.broadcasted_iota(jnp.int32, (rows, PX), 1)
@@ -66,7 +72,7 @@
 
 def blend_kernel(
     lanes_x, lanes_y, lanes_z,
-    start_ref, along_y_ref, plane_ref, weight_ref, packed_ref, out_ref,
+    start_ref, owner_ref, packed_ref, out_ref, along_y_ref, plane_ref, weight_ref,
     land0, land1, land2, land3, parts, parts_land, rims, rims_land,
     cells_out, cells_in, parts_out, parts_in, rims_out, rims_in,
 ):
@@ -129,6 +135,42 @@
         for d in far_x:
             cell_copies[c, d].start()
 
+    sub = lax.broadcasted_iota(jnp.int32, (BX, BZ), 0)
+    lane = lax.broadcasted_iota(jnp.int32, (BX, BZ), 1)
+    cell_x = place_x * BX + sub
+    cells_y = lanes_y * BY
+    starts_y = []
+    for p in range(lanes_x):
+        source = lax.rem(place_x - p + lanes_x, lanes_x)
+        code = owner_ref[source, place_y, place_z]
+        start_x, start_y, start_z = corner_of(start_ref, code, lanes_y, place_z)
+        starts_y.append(start_y)
+        shift_z = place_z * BZ - start_z
+        part = lane % (2 * RIM)
+        rim_z = jnp.where(part < RIM, part - RIM, part - RIM + BZ) + shift_z
+        along_x = profile(cell_x - start_x, PX)
+        plane_ref[p, 0] = along_x * profile(lane + shift_z, PZ)
+        plane_ref[p, 1] = along_x * profile(rim_z, PZ, lane < 2 * RIM * CLASSES)
+        row = lax.broadcasted_iota(jnp.int32, (cells_y, BZ), 0)
+        along_y_ref[p] = profile(row - start_y, PY)
+
+    weight_ref[...] = jnp.zeros(weight_ref.shape, jnp.float32)
+    cell_y = place_y * BY + lax.broadcasted_iota(jnp.int32, (BY, BZ), 0)
+
+    def weigh(code, carry):
+        for step in (-1, 0, 1):
+            layer = jnp.clip(place_z + step, 0, lanes_z - 1)
+            start_x, start_y, start_z = corner_of(start_ref, code, lanes_y, layer)
+            along = profile(cell_y - start_y, PY)
+            plane = profile(cell_x - start_x, PX) * profile(
+                place_z * BZ + lane - start_z, PZ, layer == place_z + step
+            )
+            for y in range(BY):
+                weight_ref[y] = weight_ref[y] + plane * along[y : y + 1]
+        return carry
+
+    lax.fori_loop(0, lanes_x * lanes_y, weigh, 0)
+
     def blend(c):
         kind = 0 if c < CLASSES else 1
         for d in far_y + [0]:
@@ -138,9 +180,9 @@
                 row = base + y
                 total = None
                 for p in range(lanes_x):
-                    q = jnp.clip(row - start_ref[p], 0, PY - 1)
+                    q = jnp.clip(row - starts_y[p], 0, PY - 1)
                     cells = packed_ref[c, 0, q] if p == 0 else cells_land[c][p, q]
-                    term = cells.astype(jnp.float32) * (plane_ref[p, kind] * along_y_ref[p, row])
+                    term = cells.astype(jnp.float32) * (plane_ref[p, kind] * along_y_ref[p, pl.ds(row, 1)])
                     total = term if total is None else total + term
                 parts[c, d, y] = total
                 return carry
@@ -177,7 +219,6 @@
         for d in far_y:
             part_copies[c, d].wait_recv()
 
-    lane = lax.broadcasted_iota(jnp.int32, (BX, BZ), 1)
     low_lanes = (lane < RIM) & (place_z > 0)
     high_lanes = (lane >= BZ - RIM) & (place_z < lanes_z - 1)
 
@@ -199,7 +240,7 @@
             out_ref[y, c] = powers[c] * norm
         return carry
 
-    lax.fori_loop(0, BY, finish, 0, unroll=2)
+    lax.fori_loop(0, BY, finish, 0, unroll=4)
     for copy in list(cell_copies.values()) + list(part_copies.values()) + rim_copies:
         copy.wait_send()
 
@@ -212,51 +253,24 @@
     lanes_x = lax.axis_size("gx")
     lanes_y = lax.axis_size("gy")
     lanes_z = lax.axis_size("gz")
-    place_x = lax.axis_index("gx")
-    place_y = lax.axis_index("gy")
-    place_z = lax.axis_index("gz")
-    cells_y = lanes_y * BY
-    behind = lax.rem(place_x - jnp.arange(lanes_x) + lanes_x, lanes_x)
-    codes = patch_owner[behind, place_y, place_z]
-    corners = patch_start[codes // lanes_y, codes % lanes_y, place_z]
-    place = jnp.stack([corners[0, 0], place_z * BZ - corners[0, 2], place_x])
     packed = pl.pallas_call(
-        functools.partial(pack_kernel, lanes_x),
+        functools.partial(pack_kernel, lanes_x, lanes_y),
         out_shape=jax.ShapeDtypeStruct((ROWS, lanes_x, PY, BX, BZ), jnp.bfloat16),
-        in_specs=[SMEM, VMEM],
+        in_specs=[SMEM, SMEM, VMEM],
         out_specs=VMEM,
-    )(place, patch_logits[0, 0, 0])
-
-    along_x = profile(place_x * BX + jnp.arange(BX)[None, :] - corners[:, 0:1], PX)
-    along_y = profile(jnp.arange(cells_y)[None, :] - corners[:, 1:2], PY)
-    shift = place_z * BZ - corners[:, 2:3]
-    main_z = profile(jnp.arange(BZ)[None, :] + shift, PZ)
-    j = jnp.arange(RIM)[None, :]
-    rim_z = jnp.concatenate([profile(j + shift - RIM, PZ), profile(BZ + j + shift, PZ)], axis=1)
-    rim_z = jnp.pad(jnp.tile(rim_z, (1, CLASSES)), ((0, 0), (0, BZ - 2 * RIM * CLASSES)))
-    plane = along_x[:, None, :, None] * jnp.stack([main_z, rim_z], axis=1)[:, :, None, :]
-
-    layers = jnp.clip(place_z + jnp.arange(-1, 2), 0, lanes_z - 1)
-    real = (place_z + jnp.arange(-1, 2) >= 0) & (place_z + jnp.arange(-1, 2) < lanes_z)
-    near = jnp.take(patch_start, layers, axis=2)
-    every_x = profile(place_x * BX + jnp.arange(BX) - near[..., 0:1], PX)
-    every_y = profile(place_y * BY + jnp.arange(BY) - near[..., 1:2], PY)
-    every_z = profile(place_z * BZ + jnp.arange(BZ) - near[..., 2:3], PZ)
-    every_z = jnp.where(real[None, None, :, None], every_z, 0.0)
-    every_y = every_y.reshape(-1, BY)
-    every_xz = (every_x[..., :, None] * every_z[..., None, :]).reshape(-1, BX * BZ)
-    weight = lax.dot_general(
-        every_y, every_xz, (((0,), (0,)), ((), ())), precision=lax.Precision.HIGHEST
-    ).reshape(BY, BX, BZ)
+    )(patch_start, patch_owner, patch_logits[0, 0, 0])
 
     cells_shape = (lanes_x, PY, BX, BZ)
     parts_shape = (ROWS, lanes_y, BY, BX, BZ)
     probs = pl.pallas_call(
         functools.partial(blend_kernel, lanes_x, lanes_y, lanes_z),
         out_shape=jax.ShapeDtypeStruct((BY, CLASSES, BX, BZ), jnp.float32),
-        in_specs=[SMEM, SMEM, VMEM, VMEM, VMEM],
+        in_specs=[SMEM, SMEM, VMEM],
         out_specs=VMEM,
         scratch_shapes=[
+            pltpu.VMEM((lanes_x, lanes_y * BY, BZ), jnp.float32),
+            pltpu.VMEM((lanes_x, 2, BX, BZ), jnp.float32),
+            pltpu.VMEM((BY, BX, BZ), jnp.float32),
             *[pltpu.VMEM(cells_shape, jnp.bfloat16)] * ROWS,
             pltpu.VMEM(parts_shape, jnp.float32),
             pltpu.VMEM(parts_shape, jnp.float32),
@@ -270,7 +284,7 @@
             pltpu.SemaphoreType.DMA((2,)),
         ],
         compiler_params=pltpu.CompilerParams(collective_id=0, has_side_effects=True),
-    )(corners[:, 1], along_y, plane, weight, packed)
+    )(patch_start, patch_owner, packed)
     return jnp.transpose(probs, (2, 0, 1, 3))
 
 

time: 76.4 us -> 67.6 us (0.88)
  other arithmetic: 3.62 us -> 0 us
  local copies, waits for them, and re-layouts: 7.76 us -> 4.62 us
  Pallas kernels: 63.6 us -> 62.5 us
    gather x3 -> x0, local copies, waits for them, and re-layouts: 2.57 us -> none  [the longest x1 1.32 us: per_device(): near = jnp.take(patch_start, layers, axis=2)]
    unnamed x5 -> x2, local copies, waits for them, and re-layouts: 1.49 us -> 2.81 us
    another operation x2 -> x0, other arithmetic: 1.31 us -> none  [the longest x1 1.3 us: per_device(): place = jnp.stack([corners[0, 0], place_z * BZ - corners[0, 2], place_x])]
    select_n x8 -> x0, other arithmetic: 1.18 us -> none  [the longest x5 1 us: profile(): return jnp.where(inside, values, 0.0)]
    pallas_call x1, Pallas kernels: 53.3 us -> 52.2 us  [per_device(): pl.pallas_call(functools.partial(blend_kernel, lanes_x, lanes_y, lanes_z)...]
    mul x2 -> x0, other arithmetic: 0.79 us -> none  [the longest x1 0.67 us: per_device(): along_x[:, None, :, None]]
where the time goes in v3:
time: 67.6 us; the launch traced here: 67.2 us
  Pallas kernels  62.5 us (92%)
  local copies, waits for them, and re-layouts  4.62 us (7%)
    pallas_call x1, Pallas kernels, per_device(): pl.pallas_call(functools.partial(blend_kernel, lanes_x, lanes_y, lanes_z)...  52.2 us
    pallas_call x1, Pallas kernels, per_device(): pl.pallas_call(functools.partial(pack_kernel, lanes_x, lanes_y), out_shap...  10.4 us
    unnamed x2, local copies, waits for them, and re-layouts  2.81 us
    transpose x1, local copies, waits for them, and re-layouts, per_device(): return jnp.transpose(probs, (2, 0, 1, 3))  1.82 us

profile of v3, /device:TPU:12, one launch (start us, length us, event | category | flops | bytes accessed | tf_op | source)
XLA Modules:
  0.0 67.2 jit_solution(789542736260200759)
XLA Ops:
  0.0 1.4 %copy.7.owner_ref = s32[4,4,2]{2,1,0:T(4,128)} copy(s32[4,4,2]{1,2,0:T(2,128)} %param.5) | data formatting | bytes 256 | tf_op args[2]
  1.4 1.4 %copy.6.start_ref = s32[4,4,2,3]{3,2,1,0:T(2,128)} copy(s32[4,4,2,3]{1,2,3,0:T(2,128)} %param.4) | data formatting | bytes 768 | tf_op args[1]
  2.8 10.4 %shard_map.37.packed_ref = bf16[4,4,48,8,128]{4,3,2,1,0:T(8,128)(2,1)} custom-call(s32[4,4,2,3]{3,2,1,0:T(2,128)} %copy.6.start_ref, s32[4,4,2]{2,1,0:T(4,128)} %copy.7.owner_ref, bf16[24,20736]{1,0:T(8,128)(2,1)} %bitcast.3), custom_call_target="tpu_custom_call" | custom-call | tf_op jit(solution)/shard_map/pallas_call | solution.py:256
  13.2 52.2 %shard_map.38 = f32[32,3,8,128]{3,2,1,0:T(8,128)} custom-call(s32[4,4,2,3]{3,2,1,0:T(2,128)} %copy.6.start_ref, s32[4,4,2]{2,1,0:T(4,128)} %copy.7.owner_ref, bf16[4,4,48,8,128]{4,3,2,1,0:T(8,128)(2,1)} %shard_map.37.packed_ref), custom_call_target="tpu_custom_call" | custom-call | tf_op jit(solution)/shard_map/pallas_call | solution.py:265
  65.4 1.8 %copy.8 = f32[8,32,3,128]{3,1,2,0:T(8,128)} copy(f32[8,32,3,128]{3,0,2,1:T(8,128)} %bitcast.2) | data formatting | bytes 786432 | tf_op jit(solution)/shard_map/transpose | solution.py:288

commit v4 on v3

--- a/solution.py
+++ b/solution.py
@@ -18,6 +18,7 @@
 RIM = PZ - BZ
 ROWS = CLASSES + 1
 GROUP = 8
+FOLD = PY // 2
 MESH = pl.DeviceIdType.MESH
 
 
@@ -33,12 +34,7 @@
     return [start_ref[code // lanes_y, code % lanes_y, layer, k] for k in range(3)]
 
 
-def pack_kernel(lanes_x, lanes_y, start_ref, owner_ref, logits_ref, out_ref):
-    place_x = lax.axis_index("gx")
-    place_z = lax.axis_index("gz")
-    code = owner_ref[place_x, lax.axis_index("gy"), place_z]
-    start_x, _, start_z = corner_of(start_ref, code, lanes_y, place_z)
-    shift_z = place_z * BZ - start_z
+def pick_x(lanes_x, place_x, start_x, logits_ref, cells_ref):
     rows = lanes_x * BX
     r = lax.broadcasted_iota(jnp.int32, (rows, PX), 0)
     p = lax.broadcasted_iota(jnp.int32, (rows, PX), 1)
@@ -46,40 +42,71 @@
     x = jnp.where(x >= rows, x - rows, x)
     pick = jnp.where(x - start_x == p, 1.0, 0.0).astype(jnp.bfloat16)
     width = GROUP * CLASSES * PZ
-    fill = jnp.zeros((rows, 2 * BZ - PZ), jnp.float32)
-
-    def step(g, carry):
-        lanes = pl.ds(pl.multiple_of(g * width, 128), width)
+    for g in range(PY // GROUP):
+        lanes = slice(g * width, (g + 1) * width)
         cells = jnp.dot(pick, logits_ref[:, lanes], preferred_element_type=jnp.float32)
-        for y in range(GROUP):
-            rims = None
-            for c in range(CLASSES):
-                at = (y * CLASSES + c) * PZ
-                line = jnp.concatenate([cells[:, at : at + PZ], fill], axis=1)
-                line = pltpu.roll(line, 2 * BZ - shift_z, 1)
-                main = line[:, :BZ].astype(jnp.bfloat16)
-                rim = pltpu.roll(line[:, BZ:], RIM + 2 * RIM * c, 1)
-                rims = rim if rims is None else rims + rim
-                for t in range(lanes_x):
-                    out_ref[c, t, g * GROUP + y] = main[t * BX : (t + 1) * BX]
-            rims = rims.astype(jnp.bfloat16)
+        cells_ref[:, lanes] = cells.astype(jnp.bfloat16)
+
+
+def lines_of(cells_ref, lines, source, phase):
+    k = lax.broadcasted_iota(jnp.int32, (2 * BZ, BZ), 0)
+    move = jnp.where(k - phase * RIM == source, 1.0, 0.0).astype(jnp.bfloat16)
+    starts = [line * PZ - phase * RIM for line in lines]
+    cells = jnp.concatenate([cells_ref[:, at : at + 2 * BZ] for at in starts], axis=0)
+    return jnp.dot(cells, move, preferred_element_type=jnp.float32)
+
+
+def pack_rims(lanes_x, shift_z, cells_ref, sums_ref, out_ref):
+    rows = lanes_x * BX
+    phases = BZ // RIM
+    n = lax.broadcasted_iota(jnp.int32, (2 * BZ, BZ), 1)
+    source = n + shift_z + jnp.where(n + shift_z < RIM, BZ, -RIM)
+    source = jnp.where(n < RIM, source, -4 * BZ)
+    sums_ref[...] = jnp.zeros(sums_ref.shape, jnp.float32)
+    for phase in range(phases):
+        lines = [i for i in range(PY * CLASSES) if i % phases == phase]
+        moved = lines_of(cells_ref, lines, source, phase)
+        for i, line in enumerate(lines):
+            y, c = divmod(line, CLASSES)
+            rim = moved[i * rows : (i + 1) * rows]
+            at = RIM * c + BZ // 2 * (y // FOLD)
+            rim = pltpu.roll(rim, at, 1) if at else rim
+            sums_ref[y % FOLD] = sums_ref[y % FOLD] + rim
+
+    def convert(y, carry):
+        sums = sums_ref[y].astype(jnp.bfloat16)
+        for t in range(lanes_x):
+            out_ref[t, y] = sums[t * BX : (t + 1) * BX]
+        return carry
+
+    lax.fori_loop(0, FOLD, convert, 0, unroll=2)
+
+
+def pack_class(lanes_x, shift_z, c, cells_ref, out_ref):
+    rows = lanes_x * BX
+    phases = BZ // RIM
+    source = lax.broadcasted_iota(jnp.int32, (2 * BZ, BZ), 1) + shift_z
+    for phase in range(phases):
+        ys = [y for y in range(PY) if (y * CLASSES + c) % phases == phase]
+        moved = lines_of(cells_ref, [y * CLASSES + c for y in ys], source, phase)
+        moved = moved.astype(jnp.bfloat16)
+        for i, y in enumerate(ys):
             for t in range(lanes_x):
-                out_ref[CLASSES, t, g * GROUP + y] = rims[t * BX : (t + 1) * BX]
-        return carry
-
-    lax.fori_loop(0, PY // GROUP, step, 0)
+                at = i * rows + t * BX
+                out_ref[t, y] = moved[at : at + BX]
 
 
 def blend_kernel(
     lanes_x, lanes_y, lanes_z,
-    start_ref, owner_ref, packed_ref, out_ref, along_y_ref, plane_ref, weight_ref,
-    land0, land1, land2, land3, parts, parts_land, rims, rims_land,
+    start_ref, owner_ref, logits_ref, out_ref, along_y_ref, plane_ref, weight_ref,
+    cells_ref, sums_ref, pack0, pack1, pack2, pack3, land0, land1, land2, land3, parts, parts_land, rims, rims_land,
     cells_out, cells_in, parts_out, parts_in, rims_out, rims_in,
 ):
     place_x = lax.axis_index("gx")
     place_y = lax.axis_index("gy")
     place_z = lax.axis_index("gz")
 
+    packed = (pack0, pack1, pack2, pack3)
     cells_land = (land0, land1, land2, land3)
 
     def ahead(place, d, size):
@@ -91,14 +118,18 @@
     peers += [{"gz": ahead(place_z, d, lanes_z)} for d in (1, lanes_z - 1)]
     for peer in peers:
         pl.semaphore_signal(barrier, inc=1, device_id=peer, device_id_type=MESH)
-    pl.semaphore_wait(barrier, len(peers))
+
+    code = owner_ref[place_x, place_y, place_z]
+    start_x, _, start_z = corner_of(start_ref, code, lanes_y, place_z)
+    shift_z = place_z * BZ - start_z
+    pick_x(lanes_x, place_x, start_x, logits_ref, cells_ref)
 
     order = (CLASSES,) + tuple(range(CLASSES))
     far_x = sorted(range(1, lanes_x), key=lambda d: -min(d, lanes_x - d))
     far_y = sorted(range(1, lanes_y), key=lambda d: -min(d, lanes_y - d))
     cell_copies = {
         (c, d): pltpu.make_async_remote_copy(
-            src_ref=packed_ref.at[c, d],
+            src_ref=packed[c].at[d],
             dst_ref=cells_land[c].at[d],
             send_sem=cells_out.at[c, d],
             recv_sem=cells_in.at[c, d],
@@ -132,6 +163,11 @@
         for side, d in ((0, 1), (1, lanes_z - 1))
     ]
     for c in order:
+        if c == CLASSES:
+            pack_rims(lanes_x, shift_z, cells_ref, sums_ref, packed[c])
+            pl.semaphore_wait(barrier, len(peers))
+        else:
+            pack_class(lanes_x, shift_z, c, cells_ref, packed[c])
         for d in far_x:
             cell_copies[c, d].start()
 
@@ -146,11 +182,10 @@
         start_x, start_y, start_z = corner_of(start_ref, code, lanes_y, place_z)
         starts_y.append(start_y)
         shift_z = place_z * BZ - start_z
-        part = lane % (2 * RIM)
-        rim_z = jnp.where(part < RIM, part - RIM, part - RIM + BZ) + shift_z
+        rim_z = lane % RIM + jnp.where(lane < BZ // 2, -RIM, BZ) + shift_z
         along_x = profile(cell_x - start_x, PX)
         plane_ref[p, 0] = along_x * profile(lane + shift_z, PZ)
-        plane_ref[p, 1] = along_x * profile(rim_z, PZ, lane < 2 * RIM * CLASSES)
+        plane_ref[p, 1] = along_x * profile(rim_z, PZ, lane % (BZ // 2) < RIM * CLASSES)
         row = lax.broadcasted_iota(jnp.int32, (cells_y, BZ), 0)
         along_y_ref[p] = profile(row - start_y, PY)
 
@@ -181,8 +216,15 @@
                 total = None
                 for p in range(lanes_x):
                     q = jnp.clip(row - starts_y[p], 0, PY - 1)
-                    cells = packed_ref[c, 0, q] if p == 0 else cells_land[c][p, q]
-                    term = cells.astype(jnp.float32) * (plane_ref[p, kind] * along_y_ref[p, pl.ds(row, 1)])
+                    held = packed[c] if p == 0 else cells_land[c]
+                    if c < CLASSES:
+                        cells = held[p, q].astype(jnp.float32)
+                    else:
+                        half = jnp.where(q >= FOLD, 1, 0)
+                        cells = held[p, q - half * FOLD].astype(jnp.float32)
+                        swapped = pltpu.roll(cells, BZ // 2, 1)
+                        cells = jnp.where(lane // (BZ // 2) == half, cells, swapped)
+                    term = cells * (plane_ref[p, kind] * along_y_ref[p, pl.ds(row, 1)])
                     total = term if total is None else total + term
                 parts[c, d, y] = total
                 return carry
@@ -228,8 +270,8 @@
         above = rims_land[1, y]
         scores = []
         for c in range(CLASSES):
-            low = pltpu.roll(below, BZ - (2 * RIM * c + RIM), 1)
-            high = pltpu.roll(above, BZ - RIM - 2 * RIM * c, 1)
+            low = pltpu.roll(below, BZ // 2 - RIM * c, 1)
+            high = pltpu.roll(above, BZ - RIM - RIM * c, 1)
             total = gathered(c, y) + jnp.where(low_lanes, low, 0.0)
             total = total + jnp.where(high_lanes, high, 0.0)
             scores.append(total * scale)
@@ -253,14 +295,7 @@
     lanes_x = lax.axis_size("gx")
     lanes_y = lax.axis_size("gy")
     lanes_z = lax.axis_size("gz")
-    packed = pl.pallas_call(
-        functools.partial(pack_kernel, lanes_x, lanes_y),
-        out_shape=jax.ShapeDtypeStruct((ROWS, lanes_x, PY, BX, BZ), jnp.bfloat16),
-        in_specs=[SMEM, SMEM, VMEM],
-        out_specs=VMEM,
-    )(patch_start, patch_owner, patch_logits[0, 0, 0])
-
-    cells_shape = (lanes_x, PY, BX, BZ)
+    row_shapes = [(lanes_x, PY, BX, BZ)] * CLASSES + [(lanes_x, FOLD, BX, BZ)]
     parts_shape = (ROWS, lanes_y, BY, BX, BZ)
     probs = pl.pallas_call(
         functools.partial(blend_kernel, lanes_x, lanes_y, lanes_z),
@@ -271,7 +306,9 @@
             pltpu.VMEM((lanes_x, lanes_y * BY, BZ), jnp.float32),
             pltpu.VMEM((lanes_x, 2, BX, BZ), jnp.float32),
             pltpu.VMEM((BY, BX, BZ), jnp.float32),
-            *[pltpu.VMEM(cells_shape, jnp.bfloat16)] * ROWS,
+            pltpu.VMEM((lanes_x * BX, PY * CLASSES * PZ), jnp.bfloat16),
+            pltpu.VMEM((FOLD, lanes_x * BX, BZ), jnp.float32),
+            *[pltpu.VMEM(shape, jnp.bfloat16) for shape in row_shapes * 2],
             pltpu.VMEM(parts_shape, jnp.float32),
             pltpu.VMEM(parts_shape, jnp.float32),
             pltpu.VMEM((BY, BX, BZ), jnp.float32),
@@ -284,7 +321,7 @@
             pltpu.SemaphoreType.DMA((2,)),
         ],
         compiler_params=pltpu.CompilerParams(collective_id=0, has_side_effects=True),
-    )(patch_start, patch_owner, packed)
+    )(patch_start, patch_owner, patch_logits[0, 0, 0])
     return jnp.transpose(probs, (2, 0, 1, 3))
 
 

time: 67.6 us -> 51.4 us (0.76)
  Pallas kernels: 62.5 us -> 47.1 us
  local copies, waits for them, and re-layouts: 4.62 us -> 3.94 us
    pallas_call x1 -> x0, Pallas kernels: 10.4 us -> none  [per_device(): pl.pallas_call(functools.partial(pack_kernel, lanes_x, lanes_y), out_shap...]
    pallas_call x1, Pallas kernels: 52.2 us -> 47.1 us  [per_device(): pl.pallas_call(functools.partial(blend_kernel, lanes_x, lanes_y, lanes_z)...]
    unnamed x2 -> x4, local copies, waits for them, and re-layouts: 2.81 us -> 2.12 us
where the time goes in v4:
time: 51.4 us; the launch traced here: 51.1 us
  Pallas kernels  47.1 us (92%)
  local copies, waits for them, and re-layouts  3.94 us (8%)
    pallas_call x1, Pallas kernels, per_device(): pl.pallas_call(functools.partial(blend_kernel, lanes_x, lanes_y, lanes_z)...  47.1 us
    unnamed x4, local copies, waits for them, and re-layouts  2.12 us
    transpose x1, local copies, waits for them, and re-layouts, per_device(): return jnp.transpose(probs, (2, 0, 1, 3))  1.82 us

profile of v4, /device:TPU:12, one launch (start us, length us, event | category | flops | bytes accessed | tf_op | source)
XLA Modules:
  0.0 51.1 jit_solution(15070776173026607056)
XLA Ops:
  0.0 0.0 copy-start
  0.0 1.4 %copy.5.owner_ref = s32[4,4,2]{2,1,0:T(4,128)} copy(s32[4,4,2]{1,2,0:T(2,128)} %param.5) | data formatting | bytes 256 | tf_op args[2]
  1.4 0.0 copy-done
  1.4 0.7 %copy.4.start_ref = s32[4,4,2,3]{3,2,1,0:T(2,128)} copy(s32[4,4,2,3]{1,2,3,0:T(2,128)S(1)} %copy-done) | data formatting | bytes 768 | tf_op args[1]
  2.1 47.1 %shard_map.37 = f32[32,3,8,128]{3,2,1,0:T(8,128)} custom-call(s32[4,4,2,3]{3,2,1,0:T(2,128)} %copy.4.start_ref, s32[4,4,2]{2,1,0:T(4,128)} %copy.5.owner_ref, bf16[24,20736]{1,0:T(8,128)(2,1)} %bitcast.3), custom_call_target="tpu_custom_call" | custom-call | tf_op jit(solution)/shard_map/pallas_call | solution.py:300
  49.3 1.8 %copy.6 = f32[8,32,3,128]{3,1,2,0:T(8,128)} copy(f32[8,32,3,128]{3,0,2,1:T(8,128)} %bitcast.2) | data formatting | bytes 786432 | tf_op jit(solution)/shard_map/transpose | solution.py:325
Async XLA Ops:
  0.0 1.4 %copy-start = (s32[4,4,2,3]{1,2,3,0:T(2,128)S(1)}, s32[4,4,2,3]{1,2,3,0:T(2,128)}, u32[]{:S(2)}) copy-start(s32[4,4,2,3]{1,2,3,0:T(2,128)} %param.4) | copy-start | bytes 1156

commit v5 on v4

--- a/solution.py
+++ b/solution.py
@@ -31,7 +31,7 @@
 
 
 def corner_of(start_ref, code, lanes_y, layer):
-    return [start_ref[code // lanes_y, code % lanes_y, layer, k] for k in range(3)]
+    return [start_ref[code // lanes_y, k, layer, code % lanes_y] for k in range(3)]
 
 
 def pick_x(lanes_x, place_x, start_x, logits_ref, cells_ref):
@@ -119,12 +119,12 @@
     for peer in peers:
         pl.semaphore_signal(barrier, inc=1, device_id=peer, device_id_type=MESH)
 
-    code = owner_ref[place_x, place_y, place_z]
+    code = owner_ref[place_x, place_z, place_y]
     start_x, _, start_z = corner_of(start_ref, code, lanes_y, place_z)
     shift_z = place_z * BZ - start_z
     pick_x(lanes_x, place_x, start_x, logits_ref, cells_ref)
 
-    order = (CLASSES,) + tuple(range(CLASSES))
+    order = (0, CLASSES) + tuple(range(1, CLASSES))
     far_x = sorted(range(1, lanes_x), key=lambda d: -min(d, lanes_x - d))
     far_y = sorted(range(1, lanes_y), key=lambda d: -min(d, lanes_y - d))
     cell_copies = {
@@ -165,9 +165,10 @@
     for c in order:
         if c == CLASSES:
             pack_rims(lanes_x, shift_z, cells_ref, sums_ref, packed[c])
-            pl.semaphore_wait(barrier, len(peers))
         else:
             pack_class(lanes_x, shift_z, c, cells_ref, packed[c])
+        if c == order[0]:
+            pl.semaphore_wait(barrier, len(peers))
         for d in far_x:
             cell_copies[c, d].start()
 
@@ -178,7 +179,7 @@
     starts_y = []
     for p in range(lanes_x):
         source = lax.rem(place_x - p + lanes_x, lanes_x)
-        code = owner_ref[source, place_y, place_z]
+        code = owner_ref[source, place_z, place_y]
         start_x, start_y, start_z = corner_of(start_ref, code, lanes_y, place_z)
         starts_y.append(start_y)
         shift_z = place_z * BZ - start_z
@@ -239,42 +240,28 @@
             total = total + parts_land[c, d, y]
         return total
 
-    for c in order:
-        for d in far_x:
-            cell_copies[c, d].wait_recv()
-        blend(c)
-        if c == 0:
-            for d in far_y:
-                part_copies[CLASSES, d].wait_recv()
-
-            def add_rims(y, carry):
-                rims[y] = gathered(CLASSES, y)
-                return carry
-
-            lax.fori_loop(0, BY, add_rims, 0)
-            for copy in rim_copies:
-                copy.start()
-
-    for copy in rim_copies:
-        copy.wait_recv()
-    for c in range(CLASSES):
-        for d in far_y:
-            part_copies[c, d].wait_recv()
-
     low_lanes = (lane < RIM) & (place_z > 0)
     high_lanes = (lane >= BZ - RIM) & (place_z < lanes_z - 1)
 
+    def add_rims(y, carry):
+        rims[y] = gathered(CLASSES, y)
+        return carry
+
+    def rim_of(c, y):
+        low = pltpu.roll(rims_land[0, y], BZ // 2 - RIM * c, 1)
+        high = pltpu.roll(rims_land[1, y], BZ - RIM - RIM * c, 1)
+        return jnp.where(low_lanes, low, jnp.where(high_lanes, high, 0.0))
+
+    def early(y, carry):
+        weight_ref[y] = 1.0 / weight_ref[y]
+        for c in range(CLASSES - 1):
+            parts[c, 0, y] = (gathered(c, y) + rim_of(c, y)) * weight_ref[y]
+        parts[CLASSES - 1, 0, y] = parts[CLASSES - 1, 0, y] + rim_of(CLASSES - 1, y)
+        return carry
+
     def finish(y, carry):
-        scale = 1.0 / weight_ref[y]
-        below = rims_land[0, y]
-        above = rims_land[1, y]
-        scores = []
-        for c in range(CLASSES):
-            low = pltpu.roll(below, BZ // 2 - RIM * c, 1)
-            high = pltpu.roll(above, BZ - RIM - RIM * c, 1)
-            total = gathered(c, y) + jnp.where(low_lanes, low, 0.0)
-            total = total + jnp.where(high_lanes, high, 0.0)
-            scores.append(total * scale)
+        scores = [parts[c, 0, y] for c in range(CLASSES - 1)]
+        scores.append(gathered(CLASSES - 1, y) * weight_ref[y])
         top = functools.reduce(jnp.maximum, scores)
         powers = [jnp.exp(s - top) for s in scores]
         norm = 1.0 / functools.reduce(jnp.add, powers)
@@ -282,7 +269,26 @@
             out_ref[y, c] = powers[c] * norm
         return carry
 
-    lax.fori_loop(0, BY, finish, 0, unroll=4)
+    for c in order:
+        for d in far_x:
+            cell_copies[c, d].wait_recv()
+        blend(c)
+        if c == 1:
+            for d in far_y:
+                part_copies[CLASSES, d].wait_recv()
+            lax.fori_loop(0, BY, add_rims, 0, unroll=4)
+            for copy in rim_copies:
+                copy.start()
+
+    for copy in rim_copies:
+        copy.wait_recv()
+    for c in range(CLASSES - 1):
+        for d in far_y:
+            part_copies[c, d].wait_recv()
+    lax.fori_loop(0, BY, early, 0, unroll=4)
+    for d in far_y:
+        part_copies[CLASSES - 1, d].wait_recv()
+    lax.fori_loop(0, BY, finish, 0, unroll=8)
     for copy in list(cell_copies.values()) + list(part_copies.values()) + rim_copies:
         copy.wait_send()
 
@@ -321,7 +327,11 @@
             pltpu.SemaphoreType.DMA((2,)),
         ],
         compiler_params=pltpu.CompilerParams(collective_id=0, has_side_effects=True),
-    )(patch_start, patch_owner, patch_logits[0, 0, 0])
+    )(
+        jnp.transpose(patch_start, (0, 3, 2, 1)),
+        jnp.transpose(patch_owner, (0, 2, 1)),
+        patch_logits[0, 0, 0],
+    )
     return jnp.transpose(probs, (2, 0, 1, 3))
 
 

time: 51.4 us -> 50.4 us (0.981)
  local copies, waits for them, and re-layouts: 3.94 us -> 1.82 us
  Pallas kernels: 47.1 us -> 48.4 us
    unnamed x4 -> x0, local copies, waits for them, and re-layouts: 2.12 us -> none
    pallas_call x1, Pallas kernels: 47.1 us -> 48.4 us  [per_device(): pl.pallas_call(functools.partial(blend_kernel, lanes_x, lanes_y, lanes_z)...]
where the time goes in v5:
time: 50.4 us; the launch traced here: 50.2 us
  Pallas kernels  48.4 us (96%)
  local copies, waits for them, and re-layouts  1.82 us (4%)
    pallas_call x1, Pallas kernels, per_device(): pl.pallas_call(functools.partial(blend_kernel, lanes_x, lanes_y, lanes_z)...  48.4 us
    transpose x1, local copies, waits for them, and re-layouts, per_device(): return jnp.transpose(probs, (2, 0, 1, 3))  1.82 us

profile of v5, /device:TPU:12, one launch (start us, length us, event | category | flops | bytes accessed | tf_op | source)
XLA Modules:
  0.0 50.2 jit_solution(4214785034421236385)
XLA Ops:
  0.0 48.4 %shard_map.37 = f32[32,3,8,128]{3,2,1,0:T(8,128)} custom-call(s32[4,3,2,4]{3,2,1,0:T(2,128)} %bitcast.6, s32[4,2,4]{2,1,0:T(2,128)} %bitcast.7, bf16[24,20736]{1,0:T(8,128)(2,1)} %bitcast.5), custom_call_target="tpu_custom_call" | custom-call | tf_op jit(solution)/shard_map/pallas_call | solution.py:306
  48.4 1.8 %copy.4 = f32[8,32,3,128]{3,1,2,0:T(8,128)} copy(f32[8,32,3,128]{3,0,2,1:T(8,128)} %bitcast.4) | data formatting | bytes 786432 | tf_op jit(solution)/shard_map/transpose | solution.py:335
